TPU v7x, 128 devices: a whole 4x4x4 slice. The times are simulated.
128 devices in a mesh: dp: 32 (over x, y, core), mp: 4 (over z).
Axes of the slice: x: 4, y: 4, z: 4, core: 2. Of those that a mesh axis runs over, the one named last changes fastest.
Arguments:
- grad_parts: bfloat16 [32, 4, 1024, 4096], P('dp', None, None, 'mp'), may hold values from -4000 to 4000
- master: float32 [4, 1024, 4096], P(None, 'dp', 'mp'), may hold values from -6 to 6
- first_moment: float32 [4, 1024, 4096], P(None, 'dp', 'mp'), may hold values from -4 to 4
- second_moment: float32 [4, 1024, 4096], P(None, 'dp', 'mp'), may hold values from 0.25 to 4
- left_basis: bfloat16 [4, 1024, 4096], P(None, 'dp', 'mp'), may hold values from -1 to 1, as said below
- right_basis: bfloat16 [4, 1024, 4096], P(None, 'dp', 'mp'), may hold values from -1 to 1, as said below
Outputs:
- weights: bfloat16 [4, 1024, 4096], P(None, None, 'mp')
- new_master: float32 [4, 1024, 4096], P(None, 'dp', 'mp')
- new_first: float32 [4, 1024, 4096], P(None, 'dp', 'mp')
- new_second: float32 [4, 1024, 4096], P(None, 'dp', 'mp')
Inputs may be any that keep to these rules, and one draw needn't show every extreme that they name: Each block left_basis[i, :, j * 1024 : (j + 1) * 1024] is an orthogonal 1024 x 1024 matrix up to rounding. Each block right_basis[i, :, j * 1024 : (j + 1) * 1024] is an orthogonal 1024 x 1024 matrix up to rounding.
All inputs are finite; a program needn't handle non-finite values.
Results may differ from a plain program's by a relative error of at most 0.02.
Values may be sent and summed in bfloat16 or wider, within the bound.
A program may use at most 128 MiB of HBM per device.

v0:
```python
import jax
import jax.numpy as jnp
from jax import lax
from jax.sharding import Mesh
from jax.sharding import PartitionSpec as P

D = 4096
STEP = 10
DP = ("dp_0", "dp_1", "dp_2")
DP_MP = ("dp_0", "dp_1", "dp_2", "mp")


beta_one = 0.95
beta_two = 0.95
epsilon = 1e-08
norm_epsilon = 1e-06
learning_rate = 0.3
decay_rate = 0.1


def over_axes(array, axes):
    for axis in axes:
        array = lax.psum(array, axis)
    return array


def split_up(array, dim, peers):
    before, after = (array.shape[:dim], array.shape[dim + 1 :])
    return jnp.moveaxis(array.reshape(*before, peers, -1, *after), dim, 0)


def summed_rows(array, chips, core, dim):
    sizes = (lax.axis_size(chips), lax.axis_size(core))
    parts = split_up(array, dim, sizes[0] * sizes[1])
    inside = parts.shape[1:]
    parts = parts.reshape(*sizes, *inside).swapaxes(0, 1).reshape(-1, *inside)
    parts = lax.psum_scatter(parts, core, scatter_dimension=0, tiled=True)
    return lax.psum_scatter(parts, chips, scatter_dimension=0, tiled=True)[0]


def per_device(grad_parts, master, first_moment, second_moment, left_basis, right_basis):
    gradient = lax.psum_scatter(grad_parts[0], DP, scatter_dimension=1, tiled=True).astype(
        jnp.float32
    )
    squares_sum = over_axes(jnp.sum(gradient * gradient), DP_MP)
    clip_scale = jnp.minimum(1.0, 2.0 * D / jnp.sqrt(squares_sum + norm_epsilon))
    grad_low = gradient.astype(jnp.bfloat16)
    right_full = lax.all_gather(right_basis, DP, axis=1, tiled=True)
    turned = jnp.einsum(
        "isk,ikb->isb", grad_low, right_full, preferred_element_type=jnp.float32
    ).astype(jnp.bfloat16)
    left_cols = left_basis
    raw_term = jnp.einsum("isx,isb->xib", left_cols, turned, preferred_element_type=jnp.float32)
    rotated_rows = summed_rows(
        lax.optimization_barrier(raw_term.astype(jnp.bfloat16))
        .astype(jnp.float32)
        .astype(jnp.bfloat16),
        ("dp_0", "dp_1"),
        "dp_2",
        0,
    ).astype(jnp.float32)
    rotated = jnp.transpose(rotated_rows, (1, 0, 2))
    clipped = clip_scale * rotated
    new_first = beta_one * first_moment + (1.0 - beta_one) * clipped
    new_second = beta_two * second_moment + (1.0 - beta_two) * clipped * clipped
    bias_one = 1.0 - beta_one**STEP
    bias_two = 1.0 - beta_two**STEP
    direction = (new_first / bias_one / (jnp.sqrt(new_second / bias_two) + epsilon)).astype(
        jnp.bfloat16
    )
    back_rows = jnp.einsum(
        "isb,icb->isc", direction, right_full, preferred_element_type=jnp.float32
    ).astype(jnp.bfloat16)
    left_cols = left_basis
    update = jnp.einsum(
        "isk,ikc->isc",
        left_cols,
        lax.all_gather(back_rows, DP, axis=1, tiled=True),
        preferred_element_type=jnp.float32,
    )
    new_master = master * (1.0 - learning_rate * decay_rate) - learning_rate * update
    weights = lax.all_gather(new_master.astype(jnp.bfloat16), DP, axis=1, tiled=True)
    return (weights, new_master, new_first, new_second)


def solution(mesh):
    finer = Mesh(mesh.devices.reshape(4, 4, 2, mesh.shape["mp"]), ("dp_0", "dp_1", "dp_2", "mp"))
    placed = (
        P(DP, None, None, "mp"),
        P(None, DP, "mp"),
        P(None, DP, "mp"),
        P(None, DP, "mp"),
        P(None, DP, "mp"),
        P(None, DP, "mp"),
    )
    return jax.shard_map(
        per_device,
        mesh=finer,
        in_specs=placed,
        out_specs=(P(None, None, "mp"), P(None, DP, "mp"), P(None, DP, "mp"), P(None, DP, "mp")),
        check_vma=False,
    )
```

profile of v0, /device:TPU:1, one launch (start us, length us, event | category | flops | bytes accessed | tf_op | source)
XLA Modules:
  0.0 428.3 jit_solution(16834403755977702970)
XLA Ops:
  7.2 0.0 copy-start
  7.2 0.0 reduce-scatter.6.cloned.1.call-start
  7.2 0.7 reduce-scatter.6.cloned.1.call-update
  7.9 0.0 all-gather.4.cloned.1.call-start
  8.0 0.7 all-gather.4.cloned.1.call-update
  8.7 0.0 reduce-scatter.8.cloned.1.call-start
  8.7 97.1 %reduce-scatter.6.cloned.1.call-done = bf16[4,32,1024]{2,1,0:T(8,128)(2,1)} async-done(((bf16[4,1024,1024]{2,1,0:T(8,128)(2,1)}), bf16[4,32,1024]{2,1,0:T(8,128)(2,1)}) %reduce-scatter.6.cloned.1.call-update) | async-done | bytes 262160 | tf_op jit(solution)/shard_map/reduce_scatter | solution.py:42
  105.8 56.5 %all-gather.4.cloned.1.call-done = bf16[4,1024,1024]{2,1,0:T(8,128)(2,1)} async-done(((bf16[4,32,1024]{2,1,0:T(8,128)(2,1)}), bf16[4,1024,1024]{2,1,0:T(8,128)(2,1)}) %all-gather.4.cloned.1.call-update) | async-done | bytes 8388624 | tf_op jit(solution)/shard_map/all_gather | solution.py:48
  162.3 10.8 %convert_bitcast_fusion = bf16[1024,4,1024]{0,2,1:T(8,128)(2,1)} fusion(bf16[4,32,1024]{2,1,0:T(8,128)(2,1)S(1)} %copy-done, bf16[4,32,1024]{2,1,0:T(8,128)(2,1)} %reduce-scatter.6.cloned.1.call-done, bf16[4,1024,1024]{2,1,0:T(8,128)(2,1)} %all-gather.4.cloned.1.call-done), kind=kOutput, calls=%fused_computation | convolution fusion | flops 541196288 | bytes 17301504 | tf_op jit(solution)/shard_map/isx,isb->xib/dot_general | solution.py:53
  173.2 11.4 %copy.14 = bf16[1024,4,1024]{2,0,1:T(8,128)(2,1)} copy(bf16[1024,4,1024]{0,2,1:T(8,128)(2,1)} %convert_bitcast_fusion) | data formatting | bytes 16777216 | tf_op jit(solution)/shard_map/optimization_barrier | solution.py:55
  184.6 8.6 %copy.15 = bf16[2,16,32,4,1024]{4,2,3,1,0:T(8,128)(2,1)} copy(bf16[2,16,32,4,1024]{4,2,0,1,3:T(8,128)(2,1)} %bitcast.24) | data formatting | bytes 16777216 | tf_op jit(solution)/shard_map/transpose | solution.py:36
  193.2 0.0 reduce-scatter.8.cloned.1.call-update
  193.3 0.0 reduce-scatter.10.cloned.1.call-start
  193.3 18.8 %reduce-scatter.8.cloned.1.call-done = bf16[16,32,4,1024]{3,1,2,0:T(8,128)(2,1)} async-done(((bf16[32,32,4,1024]{3,1,2,0:T(8,128)(2,1)}), bf16[16,32,4,1024]{3,1,2,0:T(8,128)(2,1)}) %reduce-scatter.8.cloned.1.call-update) | async-done | bytes 4194320 | tf_op jit(solution)/shard_map/reduce_scatter | solution.py:37
  212.1 0.0 reduce-scatter.10.cloned.1.call-update
  212.1 0.0 all-gather.6.cloned.1.call-start
  212.2 0.7 multiply_reduce_fusion
  212.9 9.1 %psum.28 = f32[]{:T(128)} all-reduce(f32[]{:T(128)} %multiply_reduce_fusion), channel_id=1, replica_groups=mesh['dp_0'=4,'dp_1'=4,'dp_2'=2,'mp'=4] {'dp_0'}, use_global_device_ids=true, to_apply=%region_2.0 | all-reduce | flops 1 | bytes 8 | tf_op jit(solution)/shard_map/psum | solution.py:23
  222.0 9.5 %psum.29 = f32[]{:T(128)} all-reduce(f32[]{:T(128)} %psum.28), channel_id=1, replica_groups=mesh['dp_0'=4,'dp_1'=4,'dp_2'=2,'mp'=4] {'dp_1'}, use_global_device_ids=true, to_apply=%region_3.0 | all-reduce | flops 1 | bytes 8 | tf_op jit(solution)/shard_map/psum | solution.py:23
  231.5 6.7 %psum.30 = f32[]{:T(128)} all-reduce(f32[]{:T(128)} %psum.29), channel_id=1, replica_groups=mesh['dp_0'=4,'dp_1'=4,'dp_2'=2,'mp'=4] {'dp_2'}, use_global_device_ids=true, to_apply=%region_4.0 | all-reduce | flops 1 | bytes 8 | tf_op jit(solution)/shard_map/psum | solution.py:23
  238.2 9.5 %psum.31 = f32[]{:T(128)} all-reduce(f32[]{:T(128)} %psum.30), channel_id=1, replica_groups=mesh['dp_0'=4,'dp_1'=4,'dp_2'=2,'mp'=4] {'mp'}, use_global_device_ids=true, to_apply=%region_5.0 | all-reduce | flops 1 | bytes 8 | tf_op jit(solution)/shard_map/psum | solution.py:23
  248.4 44.5 %reduce-scatter.10.cloned.1.call-done = bf16[1,32,4,1024]{3,1,2,0:T(8,128)(2,1)} async-done(((bf16[16,32,4,1024]{3,1,2,0:T(8,128)(2,1)}), bf16[1,32,4,1024]{3,1,2,0:T(8,128)(2,1)}) %reduce-scatter.10.cloned.1.call-update) | async-done | bytes 262160
  293.0 1.1 multiply_add_fusion
  294.1 0.0 copy-start.1
  294.1 7.0 %convolution_convert_fusion = bf16[4,32,1024]{2,1,0:T(8,128)(2,1)} fusion(bf16[4,1024,1024]{2,1,0:T(8,128)(2,1)} %all-gather.4.cloned.1.call-done, f32[4,32,1024]{2,1,0:T(8,128)S(1)} %get-tuple-element.15, f32[4,32,1024]{2,1,0:T(8,128)S(1)} %get-tuple-element.14), kind=kOutput, calls=%fused_computation.4 | convolution fusion | flops 269221888 | bytes 9699328 | tf_op jit(solution)/shard_map/isb,icb->isc/dot_general | solution.py:71
  301.2 0.0 all-gather.6.cloned.1.call-update
  301.2 0.0 all-gather.8.cloned.1.call-start
  301.2 54.2 %all-gather.6.cloned.1.call-done = bf16[4,1024,1024]{2,1,0:T(8,128)(2,1)} async-done(((bf16[4,32,1024]{2,1,0:T(8,128)(2,1)}), bf16[4,1024,1024]{2,1,0:T(8,128)(2,1)}) %all-gather.6.cloned.1.call-update) | async-done | bytes 8388624 | tf_op jit(solution)/shard_map/all_gather | solution.py:78
  355.4 5.8 %fusion.7 = (bf16[4,32,1024]{2,1,0:T(8,128)(2,1)}, f32[4,32,1024]{2,1,0:T(8,128)}) fusion(bf16[4,32,1024]{2,1,0:T(8,128)(2,1)S(1)} %copy-done, bf16[4,1024,1024]{2,1,0:T(8,128)(2,1)} %all-gather.6.cloned.1.call-done, f32[4,32,1024]{2,1,0:T(8,128)S(1)} %copy-done.6), kind=kOutput, calls=%fused_computation.16 | convolution fusion | flops 268959744 | bytes 9961472 | tf_op jit(solution)/shard_map/isk,ikc->isc/dot_general | solution.py:75
  361.2 0.0 all-gather.8.cloned.1.call-update
  361.3 52.4 %all-gather.8.cloned.1.call-done = bf16[4,1024,1024]{2,1,0:T(8,128)(2,1)} async-done(((bf16[4,32,1024]{2,1,0:T(8,128)(2,1)}), bf16[4,1024,1024]{2,1,0:T(8,128)(2,1)}) %all-gather.8.cloned.1.call-update) | async-done | bytes 8388624 | tf_op jit(solution)/shard_map/all_gather | solution.py:82
  413.7 7.8 %copy.17 = bf16[4,1024,1024]{2,1,0:T(8,128)(2,1)} copy(bf16[4,1024,1024]{2,1,0:T(8,128)(2,1)} %all-gather.8.cloned.1.call-done) | data formatting | bytes 16777216
  (12 shorter events, 0.0 us)
Async XLA Ops:
  7.2 155.2 %copy-start = (bf16[4,32,1024]{2,1,0:T(8,128)(2,1)S(1)}, bf16[4,32,1024]{2,1,0:T(8,128)(2,1)}, u32[]{:S(2)}) copy-start(bf16[4,32,1024]{2,1,0:T(8,128)(2,1)} %param.10) | copy-start | bytes 786436
  7.2 98.6 %reduce-scatter.6.cloned.1.call-start = ((), (), s32[]{:S(2)}) async-start(), calls=%async_computation.3 | async-start | bytes 8650752 | tf_op jit(solution)/shard_map/reduce_scatter | solution.py:42
  7.9 154.4 %all-gather.4.cloned.1.call-start = ((), (), s32[]{:S(2)}) async-start(), calls=%async_computation.4 | async-start | bytes 8650752 | tf_op jit(solution)/shard_map/all_gather | solution.py:48
  8.7 203.4 %reduce-scatter.8.cloned.1.call-start = ((), (), s32[]{:S(2)}) async-start(), calls=%async_computation.5 | async-start | bytes 12582912 | tf_op jit(solution)/shard_map/reduce_scatter | solution.py:37
  193.2 19.0 %copy-start.3 = (bf16[4,32,1024]{2,1,0:T(8,128)(2,1)S(1)}, bf16[4,32,1024]{2,1,0:T(8,128)(2,1)}, u32[]{:S(2)}) copy-start(bf16[4,32,1024]{2,1,0:T(8,128)(2,1)} %reduce-scatter.6.cloned.1.call-done) | copy-start | bytes 786436
  193.2 99.7 %copy-start.4 = (f32[4,32,1024]{2,1,0:T(8,128)S(1)}, f32[4,32,1024]{2,1,0:T(8,128)}, u32[]{:S(2)}) copy-start(f32[4,32,1024]{2,1,0:T(8,128)} %param.8) | copy-start | bytes 1572868
  193.2 99.7 %copy-start.5 = (f32[4,32,1024]{2,1,0:T(8,128)S(1)}, f32[4,32,1024]{2,1,0:T(8,128)}, u32[]{:S(2)}) copy-start(f32[4,32,1024]{2,1,0:T(8,128)} %param.9) | copy-start | bytes 1572868
  193.3 99.7 %reduce-scatter.10.cloned.1.call-start = ((), (), s32[]{:S(2)}) async-start(), calls=%async_computation.8 | async-start | bytes 4456448
  212.1 143.3 %copy-start.6 = (f32[4,32,1024]{2,1,0:T(8,128)S(1)}, f32[4,32,1024]{2,1,0:T(8,128)}, u32[]{:S(2)}) copy-start(f32[4,32,1024]{2,1,0:T(8,128)} %param.7) | copy-start | bytes 1572868
  212.1 143.3 %all-gather.6.cloned.1.call-start = ((), (), s32[]{:S(2)}) async-start(), calls=%async_computation.6 | async-start | bytes 8650752 | tf_op jit(solution)/shard_map/all_gather | solution.py:78
  294.1 67.1 %copy-start.1 = (f32[4,32,1024]{2,1,0:T(8,128)}, f32[4,32,1024]{2,1,0:T(8,128)S(1)}, u32[]{:S(2)}) copy-start(f32[4,32,1024]{2,1,0:T(8,128)S(1)} %get-tuple-element.14) | copy-start | bytes 1572868
  294.1 67.1 %copy-start.2 = (f32[4,32,1024]{2,1,0:T(8,128)}, f32[4,32,1024]{2,1,0:T(8,128)S(1)}, u32[]{:S(2)}) copy-start(f32[4,32,1024]{2,1,0:T(8,128)S(1)} %get-tuple-element.15) | copy-start | bytes 1572868
  301.2 112.5 %all-gather.8.cloned.1.call-start = ((), (), s32[]{:S(2)}) async-start(), calls=%async_computation.7 | async-start | bytes 8650752 | tf_op jit(solution)/shard_map/all_gather | solution.py:82
Sparse Core Ops, SparseCore 0:
  11.7 94.0 reduce-scatter.5
  108.2 54.1 all-gather.3
  193.4 18.6 reduce-scatter.7
  215.3 77.5 reduce-scatter.9
  301.3 54.0 all-gather.5
  361.4 52.2 all-gather.7
where the time goes:
time: 429 us; the launch traced here: 428 us
  waiting for transfers between devices  325 us (76%)
  blocking collectives  34.8 us (8%)
  local copies, waits for them, and re-layouts  27.8 us (6%)
  matrix products  23.7 us (6%)
  between operations  14.9 us (3%)
    reduce_scatter x1, waiting for transfers between devices, per_device(): lax.psum_scatter(grad_parts[0], DP, scatter_dimension=1, tiled=True)  97.1 us
    all_gather x1, waiting for transfers between devices, per_device(): right_full = lax.all_gather(right_basis, DP, axis=1, tiled=True)  56.5 us
    all_gather x1, waiting for transfers between devices, per_device(): lax.all_gather(back_rows, DP, axis=1, tiled=True)  54.2 us
    all_gather x1, waiting for transfers between devices, per_device(): lax.all_gather(new_master.astype(jnp.bfloat16), DP, axis=1, tiled=True)  52.4 us
    unnamed x7, waiting for transfers between devices  46 us
    psum x4, blocking collectives, over_axes(): array = lax.psum(array, axis)  34.8 us
    reduce_scatter x1, waiting for transfers between devices, summed_rows(): parts = lax.psum_scatter(parts, core, scatter_dimension=0, tiled=True)  18.8 us
    optimization_barrier x1, local copies, waits for them, and re-layouts, per_device(): lax.optimization_barrier(raw_term.astype(jnp.bfloat16)).astype(jnp.float32)  11.4 us
  transfers between devices with their start and end apart: 6, of which 6 were waited for; matrix products, arithmetic and copies ran while one was open for 0% of the time, Pallas kernels for 0%

commit v1 on v0

v1 whole, which is shorter than its diff:
```python
import functools

import jax
import jax.numpy as jnp
from jax import lax
from jax.experimental import pallas as pl
from jax.experimental.pallas import tpu as pltpu
from jax.sharding import Mesh
from jax.sharding import PartitionSpec as P

D = 4096
STEP = 10
DP = ("dp_0", "dp_1", "dp_2")
MESH = pl.DeviceIdType.MESH

beta_one = 0.95
beta_two = 0.95
epsilon = 1e-08
norm_epsilon = 1e-06
learning_rate = 0.3
decay_rate = 0.1

F32 = jnp.float32
BF16 = jnp.bfloat16
N_SEMS = 160


def kernel(
    grad,
    master,
    first,
    second,
    left,
    right,
    weights,
    new_master,
    new_first,
    new_second,
    own,
    par,
    rec_a,
    rec_b,
    right_full,
    left_rows,
    left_cols,
    turned,
    back,
    states,
    states_out,
    master_in,
    first_in,
    second_in,
    grad_low,
    direction,
    rotated,
    rotated_out,
    rotated_in,
    update_out,
    update_in,
    squares,
    send_sems,
    recv_sems,
    local_sems,
):
    x, y, c, z = [lax.axis_index(n) for n in ("dp_0", "dp_1", "dp_2", "mp")]
    is_x = c == 0
    p_a = jnp.where(is_x, x, y)
    p_b = jnp.where(is_x, y, x)
    q = 2 * x + c
    h_own = y // 2

    def plus(v, d):
        return lax.rem(v + (d % 4), 4)

    def at_a(d):
        return (jnp.where(is_x, plus(x, d), x), jnp.where(is_x, y, plus(y, d)), c, z)

    def at_b(d):
        return (jnp.where(is_x, x, plus(x, d)), jnp.where(is_x, plus(y, d), y), c, z)

    def at_x(d):
        return (plus(x, d), y, c, z)

    partner = (x, y, 1 - c, z)
    used = [0]
    sent = []

    def sem_index():
        used[0] += 1
        return used[0] - 1

    def message(src, dst, device):
        k = sem_index()
        copy = pltpu.make_async_remote_copy(
            src_ref=src,
            dst_ref=dst,
            send_sem=send_sems.at[k],
            recv_sem=recv_sems.at[k],
            device_id=device,
            device_id_type=MESH,
        )
        copy.start()
        sent.append(copy)
        return copy

    barrier = pltpu.get_barrier_semaphore()
    peers = []
    for d in range(4):
        for e in range(2):
            if d or e:
                peers.append((plus(x, d), y, lax.rem(c + e, 2), z))
            if d:
                peers.append((x, plus(y, d), lax.rem(c + e, 2), z))
    for d in range(1, 4):
        peers.append((x, y, c, plus(z, d)))
    for device in peers:
        pl.semaphore_signal(barrier, inc=1, device_id=device, device_id_type=MESH)
    pl.semaphore_wait(barrier, len(peers))

    order_a = (2, 1, 3, 0)
    k_swap = [sem_index() for _ in range(4)]

    def slab_of(a, of_x):
        return grad.at[:, a, 0] if of_x else grad.at[a, :, 1]

    def swap_copy(n, a, of_x):
        return pltpu.make_async_remote_copy(
            src_ref=slab_of(a, of_x),
            dst_ref=par.at[a],
            send_sem=send_sems.at[k_swap[n]],
            recv_sem=recv_sems.at[k_swap[n]],
            device_id=partner,
            device_id_type=MESH,
        )

    for n, d in enumerate(order_a):
        for of_x in (True, False):

            @pl.when(is_x == of_x)
            def _():
                a = plus(x if of_x else y, d)
                pltpu.make_async_copy(slab_of(a, of_x), own.at[a], local_sems.at[n]).start()

            @pl.when(is_x != of_x)
            def _():
                swap_copy(n, plus(x if of_x else y, d), of_x).start()

    def wait_slab(n, d):
        a = plus(p_a, d)
        pltpu.make_async_copy(own.at[a], own.at[a], local_sems.at[n]).wait()
        pltpu.make_async_remote_copy(
            src_ref=par.at[a],
            dst_ref=par.at[a],
            send_sem=send_sems.at[k_swap[n]],
            recv_sem=recv_sems.at[k_swap[n]],
            device_id=partner,
            device_id_type=MESH,
        ).wait_recv()
        return a

    def add_slab(a):
        @pl.loop(0, 16)
        def _(t):
            b, r = t // 4, pl.multiple_of(lax.rem(t, 4) * 32, 32)
            rows = pl.ds(r, 32)
            own[a, b, rows, :] = own[a, b, rows, :] + par[a, b, rows, :]

    strip = 2 * lax.rem(y, 2) + c

    def to_block(pairs):
        k = [[sem_index() for _ in range(4)] for _ in pairs]
        for i in range(4):
            self_case = jnp.logical_and(y == i, c == h_own)
            for m, (source, place, whole) in enumerate(pairs):

                @pl.when(self_case)
                def _():
                    pltpu.make_async_copy(source(i), place, recv_sems.at[k[m][0]]).start()

                @pl.when(jnp.logical_not(self_case))
                def _():
                    pltpu.make_async_remote_copy(
                        src_ref=source(i),
                        dst_ref=place,
                        send_sem=send_sems.at[k[m][i]],
                        recv_sem=recv_sems.at[k[m][0]],
                        device_id=(x, jnp.int32(i), h_own, z),
                        device_id_type=MESH,
                    ).start()

        def wait_recv(m):
            whole = pairs[m][2]
            pltpu.make_async_copy(whole, whole, recv_sems.at[k[m][0]]).wait()

        def wait_send():
            for i in range(4):
                self_case = jnp.logical_and(y == i, c == h_own)

                @pl.when(jnp.logical_not(self_case))
                def _():
                    for m, (source, place, whole) in enumerate(pairs):
                        pltpu.make_async_remote_copy(
                            src_ref=source(i),
                            dst_ref=place,
                            send_sem=send_sems.at[k[m][i]],
                            recv_sem=recv_sems.at[k[m][0]],
                            device_id=(x, jnp.int32(i), h_own, z),
                            device_id_type=MESH,
                        ).wait_send()

        return wait_recv, wait_send

    place_rows = pl.ds(pl.multiple_of(strip * 32, 32), 32)
    bases_recv, bases_sent = to_block(
        [
            (lambda i: right.at[i], right_full.at[2 * x + h_own, place_rows], right_full.at[q]),
            (lambda i: left.at[i], left_rows.at[place_rows], left_rows),
        ]
    )
    for n, (source, place) in enumerate(
        ((master, master_in), (first, first_in), (second, second_in))
    ):
        pltpu.make_async_copy(source, place, local_sems.at[4 + n]).start()

    def to_owners(source, place, whole):
        k = [sem_index() for _ in range(4)]

        def case(s):
            yy, cc = 2 * c + s // 2, s % 2
            self_case = jnp.logical_and(yy == y, c == cc)
            copy = pltpu.make_async_remote_copy(
                src_ref=source.at[s],
                dst_ref=place.at[y],
                send_sem=send_sems.at[k[s]],
                recv_sem=recv_sems.at[k[0]],
                device_id=(x, yy, jnp.int32(cc), z),
                device_id_type=MESH,
            )
            return self_case, copy

        for s in range(4):
            self_case, copy = case(s)

            @pl.when(self_case)
            def _():
                pltpu.make_async_copy(source.at[s], place.at[y], recv_sems.at[k[0]]).start()

            @pl.when(jnp.logical_not(self_case))
            def _():
                copy.start()

        def wait_recv():
            pltpu.make_async_copy(whole, whole, recv_sems.at[k[0]]).wait()

        def wait_send():
            for s in range(4):
                self_case, copy = case(s)

                @pl.when(jnp.logical_not(self_case))
                def _():
                    copy.wait_send()

        return wait_recv, wait_send

    def half(ref, h):
        return ref.at[pl.ds(64 * h, 64)]

    class RowGather:
        def __init__(self, buf):
            self.buf = buf
            self.left = 2 * plus(x, -1) + c
            self.right = 2 * plus(x, 1) + c
            self.far = 2 * plus(x, 2) + c

        def start(self):
            mine = self.buf.at[q]
            self.from_left = message(mine, mine, at_x(1))
            self.from_right = message(mine, mine, at_x(-1))
            self.pair = [message(mine, mine, partner)]

        def forward_left(self):
            self.from_left.wait_recv()
            piece = self.buf.at[self.left]
            self.far_0 = message(half(piece, 0), half(piece, 0), at_x(1))
            self.pair.append(message(piece, piece, partner))

        def forward_right(self):
            self.from_right.wait_recv()
            piece = self.buf.at[self.right]
            self.far_1 = message(half(piece, 1), half(piece, 1), at_x(-1))
            self.pair.append(message(piece, piece, partner))

        def forward_far(self):
            self.far_0.wait_recv()
            self.far_1.wait_recv()
            piece = self.buf.at[self.far]
            self.pair.append(message(piece, piece, partner))

        def finish(self):
            for copy in self.pair:
                copy.wait_recv()

    b_of = [plus(p_b, d) for d in order_a]
    halves = (pl.ds(0, 64), pl.ds(64, 64))

    a_far, a_next, a_prev, a_own = [plus(p_a, d) for d in order_a]
    wait_slab(0, 2)
    add_slab(a_far)
    relay_r, relay_l = [], []
    for k in range(4):
        relay_r.append(message(own.at[a_far, b_of[k], halves[0]], rec_a.at[0, k], at_a(1)))
        relay_l.append(message(own.at[a_far, b_of[k], halves[1]], rec_a.at[1, k], at_a(-1)))
    wait_slab(1, 1)
    add_slab(a_next)
    direct_r = [
        message(own.at[a_next, b_of[k], halves[1]], rec_a.at[2, k], at_a(1)) for k in range(4)
    ]
    wait_slab(2, 3)
    add_slab(a_prev)
    direct_l = [
        message(own.at[a_prev, b_of[k], halves[0]], rec_a.at[3, k], at_a(-1)) for k in range(4)
    ]

    bases_recv(0)
    gather_right = RowGather(right_full)
    gather_right.start()
    bases_recv(1)
    mine = left_cols.at[q]
    tile_copies = []
    for d in range(4):
        for e in range(2):
            xx, cc = plus(x, d), lax.rem(c + e, 2)
            columns = pl.ds(pl.multiple_of((2 * xx + cc) * 128, 128), 128)
            if d or e:
                tile_copies.append(message(left_rows.at[:, columns], mine, (xx, y, cc, z)))
            else:
                own_tile = pltpu.make_async_copy(
                    left_rows.at[:, columns], mine, local_sems.at[7]
                )
                own_tile.start()

    wait_slab(3, 0)
    add_slab(a_own)

    final_r, final_l = [], []
    for k in range(4):
        relay_r[k].wait_recv()
        own[a_next, b_of[k], 0:64, :] = own[a_next, b_of[k], 0:64, :] + rec_a[0, k]
        final_r.append(message(own.at[a_next, b_of[k], halves[0]], rec_a.at[4, k], at_a(1)))
        relay_l[k].wait_recv()
        own[a_prev, b_of[k], 64:128, :] = own[a_prev, b_of[k], 64:128, :] + rec_a[1, k]
        final_l.append(message(own.at[a_prev, b_of[k], halves[1]], rec_a.at[5, k], at_a(-1)))

    gather_right.forward_left()
    gather_right.forward_right()

    for n, ref in enumerate((master_in, first_in, second_in)):
        pltpu.make_async_copy(ref, ref, local_sems.at[4 + n]).wait()

        @pl.loop(0, 4)
        def _(i):
            states_out[i, n] = ref[i].astype(BF16)

    def sum_first(k):
        direct_l[k].wait_recv()
        final_r[k].wait_recv()
        own[a_own, b_of[k], 0:64, :] = (
            own[a_own, b_of[k], 0:64, :].astype(F32)
            + rec_a[3, k].astype(F32)
            + rec_a[4, k].astype(F32)
        ).astype(BF16)
        direct_r[k].wait_recv()
        final_l[k].wait_recv()
        own[a_own, b_of[k], 64:128, :] = (
            own[a_own, b_of[k], 64:128, :].astype(F32)
            + rec_a[2, k].astype(F32)
            + rec_a[5, k].astype(F32)
        ).astype(BF16)

    sum_first(0)
    far = own.at[a_own, b_of[0]]
    second_relay_r = message(half(far, 0), rec_b.at[0], at_b(1))
    second_relay_l = message(half(far, 1), rec_b.at[1], at_b(-1))
    sum_first(1)
    second_direct_r = message(half(own.at[a_own, b_of[1]], 1), rec_b.at[2], at_b(1))
    sum_first(2)
    second_direct_l = message(half(own.at[a_own, b_of[2]], 0), rec_b.at[3], at_b(-1))
    second_relay_r.wait_recv()
    own[a_own, b_of[1], 0:64, :] = own[a_own, b_of[1], 0:64, :] + rec_b[0]
    second_final_r = message(half(own.at[a_own, b_of[1]], 0), rec_b.at[4], at_b(1))
    second_relay_l.wait_recv()
    own[a_own, b_of[2], 64:128, :] = own[a_own, b_of[2], 64:128, :] + rec_b[1]
    second_final_l = message(half(own.at[a_own, b_of[2]], 1), rec_b.at[5], at_b(-1))
    states_recv, states_sent = to_block(
        [(lambda i: states_out.at[i], states.at[strip], states)]
    )
    sum_first(3)
    gather_right.forward_far()

    def sum_second(rows, one, two):
        total = jnp.zeros((8, 1024), F32)
        for r in range(0, 64, 16):
            at = pl.ds(rows + r, 16)
            part = pl.ds(r, 16)
            value = (
                own[a_own, p_b, at, :].astype(F32)
                + rec_b[one, part, :].astype(F32)
                + rec_b[two, part, :].astype(F32)
            )
            grad_low[at, :] = value.astype(BF16)
            total = total + (value * value).reshape(2, 8, 1024).sum(0)
        return total

    second_direct_l.wait_recv()
    second_final_r.wait_recv()
    total = sum_second(0, 3, 4)
    second_direct_r.wait_recv()
    second_final_l.wait_recv()
    total = total + sum_second(64, 2, 5)
    total = total.reshape(8, 8, 128).sum(1) if False else sum(
        total[:, 128 * k : 128 * (k + 1)] for k in range(8)
    )
    squares[0] = total
    squares_pair = message(squares.at[0], squares.at[1], partner)

    gather_right.finish()
    for n in range(4):
        columns = slice(256 * n, 256 * (n + 1))
        acc = jnp.zeros((128, 256), F32)
        for k in range(8):
            acc = acc + jnp.dot(
                grad_low[:, 128 * k : 128 * (k + 1)],
                right_full[k, :, columns],
                preferred_element_type=F32,
            )
        turned[q, :, columns] = acc.astype(BF16)
    gather_turned = RowGather(turned)
    gather_turned.start()

    def spread_squares(slot, devices):
        return [
            message(squares.at[slot], squares.at[slot + 1 + n], device)
            for n, device in enumerate(devices)
        ]

    squares_pair.wait_recv()
    squares[2] = squares[0] + squares[1]
    over_x = spread_squares(2, [at_x(d) for d in (1, 2, 3)])
    gather_turned.forward_left()
    gather_turned.forward_right()
    for copy in over_x:
        copy.wait_recv()
    squares[6] = (squares[2] + squares[3]) + (squares[4] + squares[5])
    over_y = spread_squares(6, [(x, plus(y, d), c, z) for d in (1, 2, 3)])
    for copy in over_y:
        copy.wait_recv()
    squares[10] = (squares[6] + squares[7]) + (squares[8] + squares[9])
    over_z = spread_squares(10, [(x, y, c, plus(z, d)) for d in (1, 2, 3)])
    gather_turned.forward_far()
    for copy in over_z:
        copy.wait_recv()
    total = (squares[10] + squares[11]) + (squares[12] + squares[13])
    squares_sum = jnp.sum(jnp.sum(total, axis=1, keepdims=True), axis=0, keepdims=True)
    clip_scale = jnp.minimum(1.0, 2.0 * D / jnp.sqrt(squares_sum + norm_epsilon))

    own_tile.wait()
    for copy in tile_copies:
        copy.wait_recv()
    gather_turned.finish()
    states_recv(0)
    bias_one = 1.0 - beta_one**STEP
    bias_two = 1.0 - beta_two**STEP

    def moments(clipped, m, v):
        return (
            beta_one * m + (1.0 - beta_one) * clipped,
            beta_two * v + (1.0 - beta_two) * clipped * clipped,
        )

    for n in range(4):
        columns = slice(256 * n, 256 * (n + 1))
        acc = lax.dot_general(
            left_cols[...].reshape(1024, 128),
            turned[:, :, columns].reshape(1024, 256),
            (((0,), (0,)), ((), ())),
            preferred_element_type=F32,
        )
        for s in range(4):
            rows = acc[32 * s : 32 * (s + 1)]
            rotated_out[s, :, columns] = rows.astype(BF16)
            m, v = moments(
                clip_scale * rows,
                states[s, 1, :, columns].astype(F32),
                states[s, 2, :, columns].astype(F32),
            )
            direction[32 * s : 32 * (s + 1), columns] = (
                m / bias_one / (jnp.sqrt(v / bias_two) + epsilon)
            ).astype(BF16)

    for n in range(8):
        back[q, :, 128 * n : 128 * (n + 1)] = lax.dot_general(
            direction[...],
            right_full[n],
            (((1,), (1,)), ((), ())),
            preferred_element_type=F32,
        ).astype(BF16)
    gather_back = RowGather(back)
    gather_back.start()
    rotated_recv, rotated_sent = to_owners(rotated_out, rotated_in, rotated_in)
    gather_back.forward_left()
    gather_back.forward_right()

    rotated_recv()

    @pl.loop(0, 4)
    def _(i):
        m, v = moments(clip_scale * rotated_in[i].astype(F32), first_in[i], second_in[i])
        new_first[i] = m
        new_second[i] = v

    gather_back.forward_far()
    gather_back.finish()

    def piece(a, b):
        return weights.at[jnp.where(is_x, b, a), 2 * jnp.where(is_x, a, b) + c]

    keep = 1.0 - learning_rate * decay_rate
    for n in range(4):
        columns = slice(256 * n, 256 * (n + 1))
        acc = jnp.dot(
            left_rows[...],
            back[:, :, columns].reshape(1024, 256),
            preferred_element_type=F32,
        )
        for s in range(4):
            rows = acc[32 * s : 32 * (s + 1)]
            update_out[s, :, columns] = rows.astype(BF16)
            weights[y, q, 32 * s : 32 * (s + 1), columns] = (
                states[s, 0, :, columns].astype(F32) * keep - learning_rate * rows
            ).astype(BF16)

    pair = []

    def to_pair(ref):
        pair.append(message(ref, ref, partner))

    mine = piece(p_a, p_b)
    b_from_prev = message(mine, mine, at_b(1))
    b_from_next = message(mine, mine, at_b(-1))
    a_from_prev = [message(mine, mine, at_a(1))]
    a_from_next = [message(mine, mine, at_a(-1))]
    to_pair(mine)
    update_recv, update_sent = to_owners(update_out, update_in, update_in)

    b_from_prev.wait_recv()
    got = piece(p_a, plus(p_b, -1))
    b_far_0 = message(half(got, 0), half(got, 0), at_b(1))
    a_from_prev.append(message(got, got, at_a(1)))
    a_from_next.append(message(got, got, at_a(-1)))
    to_pair(got)
    b_from_next.wait_recv()
    got = piece(p_a, plus(p_b, 1))
    b_far_1 = message(half(got, 1), half(got, 1), at_b(-1))
    a_from_prev.append(message(got, got, at_a(1)))
    a_from_next.append(message(got, got, at_a(-1)))
    to_pair(got)
    a_far = []

    def pass_on(k, b):
        a_from_prev[k].wait_recv()
        got = piece(plus(p_a, -1), b)
        far_0 = message(half(got, 0), half(got, 0), at_a(1))
        to_pair(got)
        a_from_next[k].wait_recv()
        got = piece(plus(p_a, 1), b)
        far_1 = message(half(got, 1), half(got, 1), at_a(-1))
        to_pair(got)
        a_far.append((far_0, far_1, b))

    pass_on(0, p_b)
    b_far_0.wait_recv()
    b_far_1.wait_recv()
    got = piece(p_a, plus(p_b, 2))
    a_from_prev.append(message(got, got, at_a(1)))
    a_from_next.append(message(got, got, at_a(-1)))
    to_pair(got)

    update_recv()

    @pl.loop(0, 4)
    def _(i):
        new_master[i] = master_in[i] * keep - learning_rate * update_in[i].astype(F32)

    def take_far(k):
        far_0, far_1, b = a_far[k]
        far_0.wait_recv()
        far_1.wait_recv()
        to_pair(piece(plus(p_a, 2), b))

    pass_on(1, plus(p_b, -1))
    take_far(0)
    pass_on(2, plus(p_b, 1))
    take_far(1)
    pass_on(3, plus(p_b, 2))
    take_far(2)
    take_far(3)
    for copy in pair:
        copy.wait_recv()

    for copy in sent:
        copy.wait_send()
    for n, d in enumerate(order_a):
        swap_copy(n, d, False).wait_send()
    bases_sent()
    states_sent()
    rotated_sent()
    update_sent()


def per_device(grad_parts, master, first_moment, second_moment, left_basis, right_basis):
    vmem = pl.BlockSpec(memory_space=pltpu.VMEM)
    hbm = pl.BlockSpec(memory_space=pl.ANY)
    state = jax.ShapeDtypeStruct((4, 32, 1024), F32)
    weights, new_master, new_first, new_second = pl.pallas_call(
        kernel,
        out_shape=(
            jax.ShapeDtypeStruct((4, 8, 128, 1024), BF16),
            state,
            state,
            state,
        ),
        in_specs=[hbm] * 6,
        out_specs=(vmem, vmem, vmem, vmem),
        scratch_shapes=[
            pltpu.VMEM((4, 4, 128, 1024), BF16),
            pltpu.VMEM((4, 4, 128, 1024), BF16),
            pltpu.VMEM((6, 4, 64, 1024), BF16),
            pltpu.VMEM((6, 64, 1024), BF16),
            pltpu.VMEM((8, 128, 1024), BF16),
            pltpu.VMEM((128, 1024), BF16),
            pltpu.VMEM((8, 128, 128), BF16),
            pltpu.VMEM((8, 128, 1024), BF16),
            pltpu.VMEM((8, 128, 1024), BF16),
            pltpu.VMEM((4, 3, 32, 1024), BF16),
            pltpu.VMEM((4, 3, 32, 1024), BF16),
            pltpu.VMEM((4, 32, 1024), F32),
            pltpu.VMEM((4, 32, 1024), F32),
            pltpu.VMEM((4, 32, 1024), F32),
            pltpu.VMEM((128, 1024), BF16),
            pltpu.VMEM((128, 1024), BF16),
            pltpu.VMEM((128, 1024), F32),
            pltpu.VMEM((4, 32, 1024), BF16),
            pltpu.VMEM((4, 32, 1024), BF16),
            pltpu.VMEM((4, 32, 1024), BF16),
            pltpu.VMEM((4, 32, 1024), BF16),
            pltpu.VMEM((14, 8, 128), F32),
            pltpu.SemaphoreType.DMA((N_SEMS,)),
            pltpu.SemaphoreType.DMA((N_SEMS,)),
            pltpu.SemaphoreType.DMA((8,)),
        ],
        compiler_params=pltpu.CompilerParams(
            collective_id=0, has_side_effects=True, vmem_limit_bytes=60 * 1024 * 1024
        ),
    )(
        grad_parts.reshape(4, 4, 2, 128, 1024),
        master,
        first_moment,
        second_moment,
        left_basis,
        right_basis,
    )
    return (weights.reshape(4, 1024, 1024), new_master, new_first, new_second)


def solution(mesh):
    finer = Mesh(mesh.devices.reshape(4, 4, 2, mesh.shape["mp"]), ("dp_0", "dp_1", "dp_2", "mp"))
    placed = (
        P(DP, None, None, "mp"),
        P(None, DP, "mp"),
        P(None, DP, "mp"),
        P(None, DP, "mp"),
        P(None, DP, "mp"),
        P(None, DP, "mp"),
    )
    return jax.shard_map(
        per_device,
        mesh=finer,
        in_specs=placed,
        out_specs=(P(None, None, "mp"), P(None, DP, "mp"), P(None, DP, "mp"), P(None, DP, "mp")),
        check_vma=False,
    )
```

time: 429 us -> 126 us (0.29)
  waiting for transfers between devices: 325 us -> 0 us
  Pallas kernels: 0 us -> 115 us
  blocking collectives: 34.8 us -> 0 us
  matrix products: 23.7 us -> 0 us
  local copies, waits for them, and re-layouts: 27.8 us -> 10.3 us
  between operations: 14.9 us -> 0.67 us
    all_gather x3 -> x0, waiting for transfers between devices: 163 us -> none  [the longest x1 56.5 us: per_device(): right_full = lax.all_gather(right_basis, DP, axis=1, tiled=True)]
    reduce_scatter x2 -> x0, waiting for transfers between devices: 116 us -> none  [the longest x1 97.1 us: per_device(): lax.psum_scatter(grad_parts[0], DP, scatter_dimension=1, tiled=True)]
    pallas_call x0 -> x1, Pallas kernels: none -> 115 us  [per_device(): pl.pallas_call(kernel, out_shape=(jax.ShapeDtypeStruct((4, 8, 128, 1024),...]
    unnamed x7 -> x0, waiting for transfers between devices: 46 us -> none
    psum x4 -> x0, blocking collectives: 34.8 us -> none  [over_axes(): array = lax.psum(array, axis)]
    dot_general x3 -> x0, matrix products: 23.7 us -> none  [the longest x1 10.8 us: per_device(): jnp.einsum('isx,isb->xib', left_cols, turned, preferred_element_type=jnp....]
    optimization_barrier x1 -> x0, local copies, waits for them, and re-layouts: 11.4 us -> none  [per_device(): lax.optimization_barrier(raw_term.astype(jnp.bfloat16)).astype(jnp.float32)]
    transpose x1 -> x0, local copies, waits for them, and re-layouts: 8.64 us -> none  [summed_rows(): parts = parts.reshape(*sizes, *inside).swapaxes(0, 1).reshape(-1, *inside)]
  transfers between devices with their start and end apart: 6 -> 0, of which waited for: 6 -> 0; matrix products, arithmetic and copies ran while one was open for 0% -> 0% of each run, Pallas kernels for 0% -> 0%
where the time goes in v1:
time: 126 us
  Pallas kernels  115 us (91%)
  local copies, waits for them, and re-layouts  10.3 us (8%)
    pallas_call x1, Pallas kernels, per_device(): pl.pallas_call(kernel, out_shape=(jax.ShapeDtypeStruct((4, 8, 128, 1024),...  115 us
    unnamed x10, local copies, waits for them, and re-layouts  10.3 us

profile of v1, /device:TPU:1, one launch (start us, length us, event | category | flops | bytes accessed | tf_op | source)
XLA Modules:
  0.0 125.9 jit_solution(17635567142652453647)
XLA Ops:
  0.6 114.9 %shard_map.93 = (bf16[4,8,128,1024]{3,2,1,0:T(8,128)(2,1)}, f32[4,32,1024]{2,1,0:T(8,128)}, f32[4,32,1024]{2,1,0:T(8,128)}, f32[4,32,1024]{2,1,0:T(8,128)}) custom-call(bf16[4,4,2,128,1024]{4,3,2,1,0:T(8,128)(2,1)} %bitcast.2, f32[4,32,1024]{2,1,0:T(8,128)} %master.1, f32[4,32,1024]{2,1,0:T(8,128)} %first.1, f32[4,32,1024]{2,1,0:T(8,128)} %second.1, ...), custom_call_target="tpu_custom_call" | custom-call | tf_op jit(solution)/shard_map/pallas_call | solution.py:624
  115.6 0.0 copy-start.2
  115.6 0.0 copy-start.1
  115.6 0.0 copy-start
  115.6 7.9 %copy.14 = bf16[4,1024,1024]{2,1,0:T(8,128)(2,1)} copy(bf16[4,1024,1024]{2,1,0:T(8,128)(2,1)} %bitcast.3) | data formatting | bytes 16777216
  123.5 0.0 copy-done.2
  123.5 0.8 copy.15
  124.3 0.0 copy-done.1
  124.3 0.8 copy.16
  125.1 0.0 copy-done
  125.1 0.8 copy.17
Async XLA Ops:
  115.6 7.9 %copy-start.2 = (f32[4,32,1024]{2,1,0:T(8,128)S(1)}, f32[4,32,1024]{2,1,0:T(8,128)}, u32[]{:S(2)}) copy-start(f32[4,32,1024]{2,1,0:T(8,128)} %get-tuple-element.17) | copy-start | bytes 1572868
  115.6 8.7 %copy-start.1 = (f32[4,32,1024]{2,1,0:T(8,128)S(1)}, f32[4,32,1024]{2,1,0:T(8,128)}, u32[]{:S(2)}) copy-start(f32[4,32,1024]{2,1,0:T(8,128)} %get-tuple-element.18) | copy-start | bytes 1572868
  115.6 9.5 %copy-start = (f32[4,32,1024]{2,1,0:T(8,128)S(1)}, f32[4,32,1024]{2,1,0:T(8,128)}, u32[]{:S(2)}) copy-start(f32[4,32,1024]{2,1,0:T(8,128)} %get-tuple-element.19) | copy-start | bytes 1572868

commit v2 on v1

v2 whole, which is shorter than its diff:
```python
import functools

import jax
import jax.numpy as jnp
from jax import lax
from jax.experimental import pallas as pl
from jax.experimental.pallas import tpu as pltpu
from jax.sharding import Mesh
from jax.sharding import PartitionSpec as P

D = 4096
STEP = 10
DP = ("dp_0", "dp_1", "dp_2")
MESH = pl.DeviceIdType.MESH

beta_one = 0.95
beta_two = 0.95
epsilon = 1e-08
norm_epsilon = 1e-06
learning_rate = 0.3
decay_rate = 0.1

F32 = jnp.float32
BF16 = jnp.bfloat16
N_SEMS = 200


def kernel(
    grad,
    master,
    first,
    second,
    left,
    right,
    weights,
    new_master,
    new_first,
    new_second,
    own,
    par,
    rec_a,
    rec_b,
    right_full,
    left_rows,
    left_cols,
    turned,
    back,
    moments_near,
    moments_out,
    master_near,
    master_out,
    master_in,
    first_in,
    second_in,
    grad_low,
    direction,
    rotated_out,
    rotated_in,
    update_out,
    update_in,
    squares,
    send_sems,
    recv_sems,
    local_sems,
):
    x, y, c, z = [lax.axis_index(n) for n in ("dp_0", "dp_1", "dp_2", "mp")]
    is_x = c == 0
    p_a = jnp.where(is_x, x, y)
    p_b = jnp.where(is_x, y, x)
    q = 2 * x + c
    h_own = y // 2

    def plus(v, d):
        return lax.rem(v + (d % 4), 4)

    def at_a(d):
        return (jnp.where(is_x, plus(x, d), x), jnp.where(is_x, y, plus(y, d)), c, z)

    def at_b(d):
        return (jnp.where(is_x, x, plus(x, d)), jnp.where(is_x, plus(y, d), y), c, z)

    def at_x(d):
        return (plus(x, d), y, c, z)

    partner = (x, y, 1 - c, z)
    used = [0]
    sent = []

    def sem_index():
        used[0] += 1
        return used[0] - 1

    def message(src, dst, device):
        k = sem_index()
        copy = pltpu.make_async_remote_copy(
            src_ref=src,
            dst_ref=dst,
            send_sem=send_sems.at[k],
            recv_sem=recv_sems.at[k],
            device_id=device,
            device_id_type=MESH,
        )
        copy.start()
        sent.append(copy)
        return copy

    order_a = (2, 1, 3, 0)
    k_swap = [sem_index() for _ in range(7)]
    blocks = [(0, k) for k in range(4)] + [(n, None) for n in (1, 2, 3)]

    def source_of(n, k, of_x):
        a = plus(x if of_x else y, order_a[n])
        if k is None:
            return (grad.at[:, a, 0] if of_x else grad.at[a, :, 1]), (a,)
        b = plus(y if of_x else x, order_a[k])
        return (grad.at[b, a, 0] if of_x else grad.at[a, b, 1]), (a, b)

    def swap_copy(m, of_x):
        source, place = source_of(*blocks[m], of_x)
        return pltpu.make_async_remote_copy(
            src_ref=source,
            dst_ref=par.at[place],
            send_sem=send_sems.at[k_swap[m]],
            recv_sem=recv_sems.at[k_swap[m]],
            device_id=partner,
            device_id_type=MESH,
        )

    for m in range(7):
        for of_x in (True, False):

            @pl.when(is_x == of_x)
            def _():
                source, place = source_of(*blocks[m], of_x)
                pltpu.make_async_copy(source, own.at[place], local_sems.at[m]).start()

    for n, (source, place) in enumerate(
        ((first, first_in), (second, second_in), (master, master_in))
    ):
        pltpu.make_async_copy(source, place, local_sems.at[7 + n]).start()

    barrier = pltpu.get_barrier_semaphore()
    peers = [partner]
    for d in range(1, 4):
        peers += [(plus(x, d), y, c, z), (plus(x, d), y, 1 - c, z)]
        peers += [(x, plus(y, d), c, z), (x, plus(y, d), 1 - c, z)]
        peers += [(x, y, c, plus(z, d))]
    for device in peers:
        pl.semaphore_signal(barrier, inc=1, device_id=device, device_id_type=MESH)
    pl.semaphore_wait(barrier, len(peers))

    for m in range(7):
        for of_x in (True, False):

            @pl.when(is_x != of_x)
            def _():
                swap_copy(m, of_x).start()

    def wait_part(m):
        n, k = blocks[m]
        a = plus(p_a, order_a[n])
        place = (a,) if k is None else (a, plus(p_b, order_a[k]))
        pltpu.make_async_copy(own.at[place], own.at[place], local_sems.at[m]).wait()
        pltpu.make_async_remote_copy(
            src_ref=par.at[place],
            dst_ref=par.at[place],
            send_sem=send_sems.at[k_swap[m]],
            recv_sem=recv_sems.at[k_swap[m]],
            device_id=partner,
            device_id_type=MESH,
        ).wait_recv()

    def add_part(a, b):
        @pl.loop(0, 4)
        def _(t):
            rows = pl.ds(pl.multiple_of(t * 32, 32), 32)
            own[a, b, rows, :] = own[a, b, rows, :] + par[a, b, rows, :]

    strip = 2 * lax.rem(y, 2) + c

    def to_block(source, place, whole):
        k = [sem_index() for _ in range(4)]

        def case(i):
            copy = pltpu.make_async_remote_copy(
                src_ref=source(i),
                dst_ref=place,
                send_sem=send_sems.at[k[i]],
                recv_sem=recv_sems.at[k[0]],
                device_id=(x, jnp.int32(i), h_own, z),
                device_id_type=MESH,
            )
            return jnp.logical_and(y == i, c == h_own), copy

        for i in range(4):
            self_case, copy = case(i)

            @pl.when(self_case)
            def _():
                pltpu.make_async_copy(source(i), place, recv_sems.at[k[0]]).start()

            @pl.when(jnp.logical_not(self_case))
            def _():
                copy.start()

        def wait_recv():
            pltpu.make_async_copy(whole, whole, recv_sems.at[k[0]]).wait()

        def wait_send():
            for i in range(4):
                self_case, copy = case(i)

                @pl.when(jnp.logical_not(self_case))
                def _():
                    copy.wait_send()

        return wait_recv, wait_send

    place_rows = pl.ds(pl.multiple_of(strip * 32, 32), 32)
    right_recv, right_sent = to_block(
        lambda i: right.at[i], right_full.at[2 * x + h_own, place_rows], right_full.at[q]
    )
    left_recv, left_sent = to_block(lambda i: left.at[i], left_rows.at[place_rows], left_rows)

    def to_owners(source, place, whole):
        k = [sem_index() for _ in range(4)]

        def case(s):
            yy, cc = 2 * c + s // 2, s % 2
            self_case = jnp.logical_and(yy == y, c == cc)
            copy = pltpu.make_async_remote_copy(
                src_ref=source.at[s],
                dst_ref=place.at[y],
                send_sem=send_sems.at[k[s]],
                recv_sem=recv_sems.at[k[0]],
                device_id=(x, yy, jnp.int32(cc), z),
                device_id_type=MESH,
            )
            return self_case, copy

        for s in range(4):
            self_case, copy = case(s)

            @pl.when(self_case)
            def _():
                pltpu.make_async_copy(source.at[s], place.at[y], recv_sems.at[k[0]]).start()

            @pl.when(jnp.logical_not(self_case))
            def _():
                copy.start()

        def wait_recv():
            pltpu.make_async_copy(whole, whole, recv_sems.at[k[0]]).wait()

        def wait_send():
            for s in range(4):
                self_case, copy = case(s)

                @pl.when(jnp.logical_not(self_case))
                def _():
                    copy.wait_send()

        return wait_recv, wait_send

    def half(ref, h):
        return ref.at[pl.ds(64 * h, 64)]

    class RowGather:
        def __init__(self, buf):
            self.left = buf.at[2 * plus(x, -1) + c]
            self.right = buf.at[2 * plus(x, 1) + c]
            self.far = buf.at[2 * plus(x, 2) + c]
            mine = buf.at[q]
            self.from_left = [message(half(mine, 0), half(mine, 0), at_x(1))]
            self.from_right = [message(half(mine, 1), half(mine, 1), at_x(-1))]
            self.from_left.append(message(half(mine, 1), half(mine, 1), at_x(1)))
            self.from_right.append(message(half(mine, 0), half(mine, 0), at_x(-1)))
            self.pair = [message(mine, mine, partner)]

        def pass_on(self):
            self.from_left[0].wait_recv()
            self.far_0 = message(half(self.left, 0), half(self.left, 0), at_x(1))
            self.from_right[0].wait_recv()
            self.far_1 = message(half(self.right, 1), half(self.right, 1), at_x(-1))

        def share(self):
            self.from_left[1].wait_recv()
            self.pair.append(message(self.left, self.left, partner))
            self.from_right[1].wait_recv()
            self.pair.append(message(self.right, self.right, partner))

        def share_far(self):
            self.far_0.wait_recv()
            self.pair.append(message(half(self.far, 0), half(self.far, 0), partner))
            self.far_1.wait_recv()
            self.pair.append(message(half(self.far, 1), half(self.far, 1), partner))

        def finish(self):
            for copy in self.pair:
                copy.wait_recv()

    b_of = [plus(p_b, d) for d in order_a]
    halves = (pl.ds(0, 64), pl.ds(64, 64))

    a_far, a_next, a_prev, a_own = [plus(p_a, d) for d in order_a]
    relay_r, relay_l = [], []
    for k in range(4):
        wait_part(k)
        add_part(a_far, b_of[k])
        relay_r.append(message(own.at[a_far, b_of[k], halves[0]], rec_a.at[0, k], at_a(1)))
        relay_l.append(message(own.at[a_far, b_of[k], halves[1]], rec_a.at[1, k], at_a(-1)))
    right_recv()
    gather_right = RowGather(right_full)
    wait_part(4)
    direct_r, direct_l = [], []
    for k in range(4):
        add_part(a_next, b_of[k])
        direct_r.append(message(own.at[a_next, b_of[k], halves[1]], rec_a.at[2, k], at_a(1)))
    wait_part(5)
    for k in range(4):
        add_part(a_prev, b_of[k])
        direct_l.append(message(own.at[a_prev, b_of[k], halves[0]], rec_a.at[3, k], at_a(-1)))
    left_recv()
    mine = left_cols.at[q]
    tile_copies = []
    for d in range(4):
        for e in range(2):
            xx, cc = plus(x, d), lax.rem(c + e, 2)
            columns = pl.ds(pl.multiple_of((2 * xx + cc) * 128, 128), 128)
            if d or e:
                tile_copies.append(message(left_rows.at[:, columns], mine, (xx, y, cc, z)))
            else:
                own_tile = pltpu.make_async_copy(
                    left_rows.at[:, columns], mine, local_sems.at[10]
                )
                own_tile.start()

    wait_part(6)
    for k in range(4):
        add_part(a_own, b_of[k])

    final_r, final_l = [], []
    for k in range(4):
        relay_r[k].wait_recv()
        own[a_next, b_of[k], 0:64, :] = own[a_next, b_of[k], 0:64, :] + rec_a[0, k]
        final_r.append(message(own.at[a_next, b_of[k], halves[0]], rec_a.at[4, k], at_a(1)))
        relay_l[k].wait_recv()
        own[a_prev, b_of[k], 64:128, :] = own[a_prev, b_of[k], 64:128, :] + rec_a[1, k]
        final_l.append(message(own.at[a_prev, b_of[k], halves[1]], rec_a.at[5, k], at_a(-1)))

    gather_right.pass_on()
    gather_right.share()

    for n, (ref, packed, m) in enumerate(
        ((first_in, moments_out, 0), (second_in, moments_out, 1), (master_in, master_out, None))
    ):
        pltpu.make_async_copy(ref, ref, local_sems.at[7 + n]).wait()

        @pl.loop(0, 4)
        def _(i):
            if m is None:
                packed[i] = ref[i].astype(BF16)
            else:
                packed[i, m] = ref[i].astype(BF16)

    def sum_first(k):
        direct_l[k].wait_recv()
        final_r[k].wait_recv()
        own[a_own, b_of[k], 0:64, :] = (
            own[a_own, b_of[k], 0:64, :].astype(F32)
            + rec_a[3, k].astype(F32)
            + rec_a[4, k].astype(F32)
        ).astype(BF16)
        direct_r[k].wait_recv()
        final_l[k].wait_recv()
        own[a_own, b_of[k], 64:128, :] = (
            own[a_own, b_of[k], 64:128, :].astype(F32)
            + rec_a[2, k].astype(F32)
            + rec_a[5, k].astype(F32)
        ).astype(BF16)

    sum_first(0)
    far = own.at[a_own, b_of[0]]
    second_relay_r = message(half(far, 0), rec_b.at[0], at_b(1))
    second_relay_l = message(half(far, 1), rec_b.at[1], at_b(-1))
    sum_first(1)
    second_direct_r = message(half(own.at[a_own, b_of[1]], 1), rec_b.at[2], at_b(1))
    sum_first(2)
    second_direct_l = message(half(own.at[a_own, b_of[2]], 0), rec_b.at[3], at_b(-1))
    second_relay_r.wait_recv()
    own[a_own, b_of[1], 0:64, :] = own[a_own, b_of[1], 0:64, :] + rec_b[0]
    second_final_r = message(half(own.at[a_own, b_of[1]], 0), rec_b.at[4], at_b(1))
    second_relay_l.wait_recv()
    own[a_own, b_of[2], 64:128, :] = own[a_own, b_of[2], 64:128, :] + rec_b[1]
    second_final_l = message(half(own.at[a_own, b_of[2]], 1), rec_b.at[5], at_b(-1))
    moments_recv, moments_sent = to_block(
        lambda i: moments_out.at[i], moments_near.at[strip], moments_near
    )
    sum_first(3)
    gather_right.share_far()

    def sum_second(rows, one, two):
        total = jnp.zeros((8, 1024), F32)
        for r in range(0, 64, 16):
            at = pl.ds(rows + r, 16)
            part = pl.ds(r, 16)
            value = (
                own[a_own, p_b, at, :].astype(F32)
                + rec_b[one, part, :].astype(F32)
                + rec_b[two, part, :].astype(F32)
            )
            grad_low[at, :] = value.astype(BF16)
            total = total + (value * value).reshape(2, 8, 1024).sum(0)
        return total

    second_direct_l.wait_recv()
    second_final_r.wait_recv()
    total = sum_second(0, 3, 4)
    second_direct_r.wait_recv()
    second_final_l.wait_recv()
    total = total + sum_second(64, 2, 5)
    squares[0] = sum(total[:, 128 * k : 128 * (k + 1)] for k in range(8))
    over_row = [message(squares.at[0], squares.at[1], partner)]
    for d in (1, 2, 3):
        for cc in (c, 1 - c):
            place = squares.at[len(over_row) + 1]
            over_row.append(message(squares.at[0], place, (plus(x, d), y, cc, z)))

    gather_right.finish()
    for n in range(4):
        columns = slice(256 * n, 256 * (n + 1))
        acc = jnp.zeros((128, 256), F32)
        for k in range(8):
            acc = acc + jnp.dot(
                grad_low[:, 128 * k : 128 * (k + 1)],
                right_full[k, :, columns],
                preferred_element_type=F32,
            )
        turned[q, :, columns] = acc.astype(BF16)
    gather_turned = RowGather(turned)
    for copy in over_row:
        copy.wait_recv()
    squares[8] = sum(squares[n] for n in range(8))
    over_y = [
        message(squares.at[8], squares.at[8 + d], (x, plus(y, d), c, z)) for d in (1, 2, 3)
    ]
    master_recv, master_sent = to_block(
        lambda i: master_out.at[i], master_near.at[strip], master_near
    )
    gather_turned.pass_on()
    for copy in over_y:
        copy.wait_recv()
    squares[12] = sum(squares[n] for n in range(8, 12))
    over_z = [
        message(squares.at[12], squares.at[12 + d], (x, y, c, plus(z, d))) for d in (1, 2, 3)
    ]
    gather_turned.share()
    gather_turned.share_far()
    for copy in over_z:
        copy.wait_recv()
    total = sum(squares[n] for n in range(12, 16))
    squares_sum = jnp.sum(jnp.sum(total, axis=1, keepdims=True), axis=0, keepdims=True)
    clip_scale = jnp.minimum(1.0, 2.0 * D / jnp.sqrt(squares_sum + norm_epsilon))

    own_tile.wait()
    for copy in tile_copies:
        copy.wait_recv()
    gather_turned.finish()
    moments_recv()
    bias_one = 1.0 - beta_one**STEP
    bias_two = 1.0 - beta_two**STEP

    def moments(clipped, m, v):
        return (
            beta_one * m + (1.0 - beta_one) * clipped,
            beta_two * v + (1.0 - beta_two) * clipped * clipped,
        )

    for n in range(4):
        columns = slice(256 * n, 256 * (n + 1))
        acc = lax.dot_general(
            left_cols[...].reshape(1024, 128),
            turned[:, :, columns].reshape(1024, 256),
            (((0,), (0,)), ((), ())),
            preferred_element_type=F32,
        )
        for s in range(4):
            rows = acc[32 * s : 32 * (s + 1)]
            rotated_out[s, :, columns] = rows.astype(BF16)
            m, v = moments(
                clip_scale * rows,
                moments_near[s, 0, :, columns].astype(F32),
                moments_near[s, 1, :, columns].astype(F32),
            )
            direction[32 * s : 32 * (s + 1), columns] = (
                m / bias_one / (jnp.sqrt(v / bias_two) + epsilon)
            ).astype(BF16)

    for n in range(8):
        back[q, :, 128 * n : 128 * (n + 1)] = lax.dot_general(
            direction[...],
            right_full[n],
            (((1,), (1,)), ((), ())),
            preferred_element_type=F32,
        ).astype(BF16)
    gather_back = RowGather(back)
    rotated_recv, rotated_sent = to_owners(rotated_out, rotated_in, rotated_in)
    gather_back.pass_on()
    gather_back.share()

    rotated_recv()

    @pl.loop(0, 4)
    def _(i):
        m, v = moments(clip_scale * rotated_in[i].astype(F32), first_in[i], second_in[i])
        new_first[i] = m
        new_second[i] = v

    gather_back.share_far()
    gather_back.finish()
    master_recv()

    def piece(a, b):
        return weights.at[jnp.where(is_x, b, a), 2 * jnp.where(is_x, a, b) + c]

    keep = 1.0 - learning_rate * decay_rate
    for n in range(4):
        columns = slice(256 * n, 256 * (n + 1))
        acc = jnp.dot(
            left_rows[...],
            back[:, :, columns].reshape(1024, 256),
            preferred_element_type=F32,
        )
        for s in range(4):
            rows = acc[32 * s : 32 * (s + 1)]
            update_out[s, :, columns] = rows.astype(BF16)
            weights[y, q, 32 * s : 32 * (s + 1), columns] = (
                master_near[s, :, columns].astype(F32) * keep - learning_rate * rows
            ).astype(BF16)

    pair = []

    def to_pair(ref):
        pair.append(message(ref, ref, partner))

    def spread(ref, there, back_there):
        up = [message(half(ref, 0), half(ref, 0), there)]
        down = [message(half(ref, 1), half(ref, 1), back_there)]
        up.append(message(half(ref, 1), half(ref, 1), there))
        down.append(message(half(ref, 0), half(ref, 0), back_there))
        return up, down

    a_legs = []

    def spread_a(b):
        got = piece(p_a, b)
        a_legs.append((b, *spread(got, at_a(1), at_a(-1))))
        to_pair(got)

    mine = piece(p_a, p_b)
    b_up, b_down = spread(mine, at_b(1), at_b(-1))
    spread_a(p_b)
    update_recv, update_sent = to_owners(update_out, update_in, update_in)

    def relay(prev, following, up, down, there, back_there):
        up[0].wait_recv()
        far_0 = message(half(prev, 0), half(prev, 0), there)
        down[0].wait_recv()
        far_1 = message(half(following, 1), half(following, 1), back_there)
        return far_0, far_1

    b_prev, b_next, b_far = [plus(p_b, d) for d in (-1, 1, 2)]
    b_fars = relay(piece(p_a, b_prev), piece(p_a, b_next), b_up, b_down, at_b(1), at_b(-1))
    fars = []

    def relay_a(n):
        b, up, down = a_legs[n]
        fars.append(
            relay(piece(a_prev, b), piece(a_next, b), up, down, at_a(1), at_a(-1))
        )

    def share_a(n):
        b, up, down = a_legs[n]
        up[1].wait_recv()
        to_pair(piece(a_prev, b))
        down[1].wait_recv()
        to_pair(piece(a_next, b))

    def share_far_a(n):
        far_0, far_1 = fars[n]
        got = piece(a_far, a_legs[n][0])
        far_0.wait_recv()
        to_pair(half(got, 0))
        far_1.wait_recv()
        to_pair(half(got, 1))

    relay_a(0)
    b_up[1].wait_recv()
    spread_a(b_prev)
    b_down[1].wait_recv()
    spread_a(b_next)
    share_a(0)
    b_fars[0].wait_recv()
    b_fars[1].wait_recv()
    spread_a(b_far)
    update_recv()

    @pl.loop(0, 4)
    def _(i):
        new_master[i] = master_in[i] * keep - learning_rate * update_in[i].astype(F32)

    relay_a(1)
    share_far_a(0)
    share_a(1)
    relay_a(2)
    share_far_a(1)
    share_a(2)
    relay_a(3)
    share_far_a(2)
    share_a(3)
    share_far_a(3)
    for copy in pair:
        copy.wait_recv()

    for copy in sent:
        copy.wait_send()
    for m in range(7):
        swap_copy(m, False).wait_send()
    right_sent()
    left_sent()
    moments_sent()
    master_sent()
    rotated_sent()
    update_sent()


def write_kernel(a, b, c, d, a_out, b_out, c_out, d_out, sems):
    copies = [pltpu.make_async_copy(a.at[i], a_out.at[i], sems.at[i]) for i in range(4)]
    for n, (source, place) in enumerate(((b, b_out), (c, c_out), (d, d_out))):
        copies.append(pltpu.make_async_copy(source, place, sems.at[4 + n]))
    for copy in copies:
        copy.start()
    for copy in copies:
        copy.wait()


def per_device(grad_parts, master, first_moment, second_moment, left_basis, right_basis):
    vmem = pl.BlockSpec(memory_space=pltpu.VMEM)
    hbm = pl.BlockSpec(memory_space=pltpu.HBM)
    state = pltpu.VMEM((4, 32, 1024), F32)
    outputs = pl.pallas_call(
        kernel,
        out_shape=(
            pltpu.VMEM((4, 8, 128, 1024), BF16),
            state,
            state,
            state,
        ),
        in_specs=[hbm] * 6,
        out_specs=(vmem, vmem, vmem, vmem),
        scratch_shapes=[
            pltpu.VMEM((4, 4, 128, 1024), BF16),
            pltpu.VMEM((4, 4, 128, 1024), BF16),
            pltpu.VMEM((6, 4, 64, 1024), BF16),
            pltpu.VMEM((6, 64, 1024), BF16),
            pltpu.VMEM((8, 128, 1024), BF16),
            pltpu.VMEM((128, 1024), BF16),
            pltpu.VMEM((8, 128, 128), BF16),
            pltpu.VMEM((8, 128, 1024), BF16),
            pltpu.VMEM((8, 128, 1024), BF16),
            pltpu.VMEM((4, 2, 32, 1024), BF16),
            pltpu.VMEM((4, 2, 32, 1024), BF16),
            pltpu.VMEM((4, 32, 1024), BF16),
            pltpu.VMEM((4, 32, 1024), BF16),
            pltpu.VMEM((4, 32, 1024), F32),
            pltpu.VMEM((4, 32, 1024), F32),
            pltpu.VMEM((4, 32, 1024), F32),
            pltpu.VMEM((128, 1024), BF16),
            pltpu.VMEM((128, 1024), BF16),
            pltpu.VMEM((4, 32, 1024), BF16),
            pltpu.VMEM((4, 32, 1024), BF16),
            pltpu.VMEM((4, 32, 1024), BF16),
            pltpu.VMEM((4, 32, 1024), BF16),
            pltpu.VMEM((16, 8, 128), F32),
            pltpu.SemaphoreType.DMA((N_SEMS,)),
            pltpu.SemaphoreType.DMA((N_SEMS,)),
            pltpu.SemaphoreType.DMA((11,)),
        ],
        compiler_params=pltpu.CompilerParams(
            collective_id=0, has_side_effects=True, vmem_limit_bytes=32 * 1024 * 1024
        ),
    )(
        *(
            pltpu.with_memory_space_constraint(array, pltpu.HBM)
            for array in (
                grad_parts.reshape(4, 4, 2, 128, 1024),
                master,
                first_moment,
                second_moment,
                left_basis,
                right_basis,
            )
        )
    )
    state = jax.ShapeDtypeStruct((4, 32, 1024), F32)
    weights, new_master, new_first, new_second = pl.pallas_call(
        write_kernel,
        out_shape=(jax.ShapeDtypeStruct((4, 8, 128, 1024), BF16), state, state, state),
        in_specs=[vmem] * 4,
        out_specs=(hbm, hbm, hbm, hbm),
        scratch_shapes=[pltpu.SemaphoreType.DMA((7,))],
        compiler_params=pltpu.CompilerParams(vmem_limit_bytes=4 * 1024 * 1024),
    )(*(pltpu.with_memory_space_constraint(array, pltpu.VMEM) for array in outputs))
    return (weights.reshape(4, 1024, 1024), new_master, new_first, new_second)


def solution(mesh):
    finer = Mesh(mesh.devices.reshape(4, 4, 2, mesh.shape["mp"]), ("dp_0", "dp_1", "dp_2", "mp"))
    placed = (
        P(DP, None, None, "mp"),
        P(None, DP, "mp"),
        P(None, DP, "mp"),
        P(None, DP, "mp"),
        P(None, DP, "mp"),
        P(None, DP, "mp"),
    )
    return jax.shard_map(
        per_device,
        mesh=finer,
        in_specs=placed,
        out_specs=(P(None, None, "mp"), P(None, DP, "mp"), P(None, DP, "mp"), P(None, DP, "mp")),
        check_vma=False,
    )
```

time: 126 us -> 110 us (0.87)
  local copies, waits for them, and re-layouts: 10.3 us -> 0 us
  Pallas kernels: 115 us -> 110 us
    unnamed x10 -> x0, local copies, waits for them, and re-layouts: 10.3 us -> none
    pallas_call x1 -> x2, Pallas kernels: 115 us -> 110 us  [the longest x1 106 us: per_device(): pl.pallas_call(kernel, out_shape=(pltpu.VMEM((4, 8, 128, 1024), BF16), st...]
where the time goes in v2:
time: 110 us
  Pallas kernels  110 us (100%)
    pallas_call x1, Pallas kernels, per_device(): pl.pallas_call(kernel, out_shape=(pltpu.VMEM((4, 8, 128, 1024), BF16), st...  106 us
    pallas_call x1, Pallas kernels, per_device(): pl.pallas_call(write_kernel, out_shape=(jax.ShapeDtypeStruct((4, 8, 128,...  3.81 us

profile of v2, /device:TPU:1, one launch (start us, length us, event | category | flops | bytes accessed | tf_op | source)
XLA Modules:
  0.0 110.1 jit_solution(11955993095673914672)
XLA Ops:
  0.6 105.7 %shard_map.93 = (bf16[4,8,128,1024]{3,2,1,0:T(8,128)(2,1)S(1)}, f32[4,32,1024]{2,1,0:T(8,128)S(1)}, f32[4,32,1024]{2,1,0:T(8,128)S(1)}, f32[4,32,1024]{2,1,0:T(8,128)S(1)}) custom-call(bf16[4,4,2,128,1024]{4,3,2,1,0:T(8,128)(2,1)} %bitcast.2, f32[4,32,1024]{2,1,0:T(8,128)} %master.1, f32[4,32,1024]{2,1,0:T(8,128)} %first.1, f32[4,32,1024]{2,1,0:T(8,128)} %second.1, ...), custom_call_target="tpu_custom_call" | custom-call | tf_op jit(solution)/shard_map/pallas_call | solution.py:651
  106.3 3.8 %shard_map.94 = (bf16[4,8,128,1024]{3,2,1,0:T(8,128)(2,1)}, f32[4,32,1024]{2,1,0:T(8,128)}, f32[4,32,1024]{2,1,0:T(8,128)}, f32[4,32,1024]{2,1,0:T(8,128)}) custom-call(bf16[4,8,128,1024]{3,2,1,0:T(8,128)(2,1)S(1)} %get-tuple-element.12.a, f32[4,32,1024]{2,1,0:T(8,128)S(1)} %get-tuple-element.13.b, f32[4,32,1024]{2,1,0:T(8,128)S(1)} %get-tuple-element.14.c, ...), custom_call_target="tpu_custom_call" | custom-call | tf_op jit(solution)/shard_map/pallas_call | solution.py:706

commit v3 on v2

v3 whole, which is shorter than its diff:
```python
import math

import jax
import jax.numpy as jnp
from jax import lax
from jax.experimental import pallas as pl
from jax.experimental.pallas import tpu as pltpu
from jax.sharding import Mesh
from jax.sharding import PartitionSpec as P

D = 4096
STEP = 10
DP = ("dp_0", "dp_1", "dp_2")
MESH = pl.DeviceIdType.MESH

beta_one = 0.95
beta_two = 0.95
epsilon = 1e-08
norm_epsilon = 1e-06
learning_rate = 0.3
decay_rate = 0.1

F32 = jnp.float32
BF16 = jnp.bfloat16
N_SENDS = 24
N_ARRIVALS = 70


def kernel(
    grad,
    master,
    first,
    second,
    left,
    right,
    weights,
    new_master,
    new_first,
    new_second,
    own,
    par,
    rec_a,
    rec_b,
    right_full,
    left_rows,
    left_cols,
    turned,
    back,
    moments_near,
    moments_out,
    master_near,
    master_out,
    master_in,
    first_in,
    second_in,
    grad_low,
    direction,
    rotated_out,
    rotated_in,
    sums,
    squares,
    send_sems,
    recv_sems,
    local_sems,
):
    x, y, c, z = [lax.axis_index(n) for n in ("dp_0", "dp_1", "dp_2", "mp")]
    is_x = c == 0
    p_a = jnp.where(is_x, x, y)
    p_b = jnp.where(is_x, y, x)
    q = 2 * x + c
    h_own = y // 2

    def plus(v, d):
        return lax.rem(v + (d % 4), 4)

    def at_a(d):
        return (jnp.where(is_x, plus(x, d), x), jnp.where(is_x, y, plus(y, d)), c, z)

    def at_b(d):
        return (jnp.where(is_x, x, plus(x, d)), jnp.where(is_x, plus(y, d), y), c, z)

    def at_x(d):
        return (plus(x, d), y, c, z)

    partner = (x, y, 1 - c, z)
    used_send, used_recv = [0], [0]

    def next_index(used):
        used[0] += 1
        return used[0] - 1

    def bytes_of(ref):
        return math.prod(ref.shape) * (4 if ref.dtype == F32 else 2)

    def wait_bytes(total, sem):
        rows, pieces = total // 2048, total // (256 * 1024)
        if rows < 32:
            ref = squares.at[pl.ds(0, total // 4096)]
        elif rows <= 128:
            ref = right_full.at[0, pl.ds(0, rows)]
        elif rows % 128 == 0 and pieces <= 8:
            ref = right_full.at[pl.ds(0, pieces)]
        elif rows % 64 == 0 and rows <= 512:
            ref = right_full.at[pl.ds(0, rows // 64), pl.ds(0, 64)]
        else:
            ref = own.at[pl.ds(0, pieces // 4)]
        assert bytes_of(ref) == total, total
        pltpu.make_async_copy(ref, ref, sem).wait()

    class Arrivals:
        def __init__(self):
            self.index = next_index(used_recv)
            self.total = 0

        def wait_recv(self):
            wait_bytes(self.total, recv_sems.at[self.index])

    send_lots = {}

    def send_index(size):
        lots = send_lots.setdefault(size, [])
        if not lots or lots[-1][1] == 8:
            lots.append([next_index(used_send), 0])
        lots[-1][1] += 1
        return lots[-1][0]

    def message(src, dst, device, arrivals=None):
        arrivals = Arrivals() if arrivals is None else arrivals
        arrivals.total += bytes_of(src)
        pltpu.make_async_remote_copy(
            src_ref=src,
            dst_ref=dst,
            send_sem=send_sems.at[send_index(bytes_of(src))],
            recv_sem=recv_sems.at[arrivals.index],
            device_id=device,
            device_id_type=MESH,
        ).start()
        return arrivals

    order_a = (2, 1, 3, 0)
    k_swap = [next_index(used_recv) for _ in range(7)]
    swap_sent = [next_index(used_send) for _ in range(2)]
    blocks = [(0, k) for k in range(4)] + [(n, None) for n in (1, 2, 3)]

    def source_of(n, k, of_x):
        a = plus(x if of_x else y, order_a[n])
        if k is None:
            return (grad.at[:, a, 0] if of_x else grad.at[a, :, 1]), (a,)
        b = plus(y if of_x else x, order_a[k])
        return (grad.at[b, a, 0] if of_x else grad.at[a, b, 1]), (a, b)

    def swap_copy(m, of_x):
        source, place = source_of(*blocks[m], of_x)
        return pltpu.make_async_remote_copy(
            src_ref=source,
            dst_ref=par.at[place],
            send_sem=send_sems.at[swap_sent[m // 4]],
            recv_sem=recv_sems.at[k_swap[m]],
            device_id=partner,
            device_id_type=MESH,
        )

    for m in range(7):
        for of_x in (True, False):

            @pl.when(is_x == of_x)
            def _():
                source, place = source_of(*blocks[m], of_x)
                pltpu.make_async_copy(source, own.at[place], local_sems.at[m]).start()

    for n, (source, place) in enumerate(
        ((first, first_in), (second, second_in), (master, master_in))
    ):
        pltpu.make_async_copy(source, place, local_sems.at[7 + n]).start()

    barrier = pltpu.get_barrier_semaphore()
    peers = [partner]
    for d in range(1, 4):
        peers += [(plus(x, d), y, c, z), (plus(x, d), y, 1 - c, z)]
        peers += [(x, plus(y, d), c, z), (x, plus(y, d), 1 - c, z)]
        peers += [(x, y, c, plus(z, d))]
    for device in peers:
        pl.semaphore_signal(barrier, inc=1, device_id=device, device_id_type=MESH)
    pl.semaphore_wait(barrier, len(peers))

    for m in range(7):
        for of_x in (True, False):

            @pl.when(is_x != of_x)
            def _():
                swap_copy(m, of_x).start()

    def wait_part(m):
        n, k = blocks[m]
        a = plus(p_a, order_a[n])
        place = (a,) if k is None else (a, plus(p_b, order_a[k]))
        pltpu.make_async_copy(own.at[place], own.at[place], local_sems.at[m]).wait()
        pltpu.make_async_copy(par.at[place], par.at[place], recv_sems.at[k_swap[m]]).wait()

    def add_part(a, b):
        @pl.loop(0, 4)
        def _(t):
            rows = pl.ds(pl.multiple_of(t * 32, 32), 32)
            own[a, b, rows, :] = own[a, b, rows, :] + par[a, b, rows, :]

    strip = 2 * lax.rem(y, 2) + c

    def wait_sent(one_stays, size, index):
        def wait_send():
            for copies, condition in ((3, one_stays), (4, jnp.logical_not(one_stays))):

                @pl.when(condition)
                def _():
                    wait_bytes(copies * size, send_sems.at[index])

        return wait_send

    def to_block(source, place, whole):
        arrived, left_here = next_index(used_recv), next_index(used_send)
        for i in range(4):
            self_case = jnp.logical_and(y == i, c == h_own)

            @pl.when(self_case)
            def _():
                pltpu.make_async_copy(source(i), place, recv_sems.at[arrived]).start()

            @pl.when(jnp.logical_not(self_case))
            def _():
                pltpu.make_async_remote_copy(
                    src_ref=source(i),
                    dst_ref=place,
                    send_sem=send_sems.at[left_here],
                    recv_sem=recv_sems.at[arrived],
                    device_id=(x, jnp.int32(i), h_own, z),
                    device_id_type=MESH,
                ).start()

        def wait_recv():
            pltpu.make_async_copy(whole, whole, recv_sems.at[arrived]).wait()

        return wait_recv, wait_sent(c == h_own, bytes_of(place), left_here)

    place_rows = pl.ds(pl.multiple_of(strip * 32, 32), 32)
    right_recv, right_sent = to_block(
        lambda i: right.at[i], right_full.at[2 * x + h_own, place_rows], right_full.at[q]
    )
    left_recv, left_sent = to_block(lambda i: left.at[i], left_rows.at[place_rows], left_rows)

    def to_owners(source, place, whole):
        arrived, left_here = next_index(used_recv), next_index(used_send)
        for s in range(4):
            yy, cc = 2 * c + s // 2, s % 2
            self_case = jnp.logical_and(yy == y, c == cc)

            @pl.when(self_case)
            def _():
                pltpu.make_async_copy(
                    source.at[s], place.at[y], recv_sems.at[arrived]
                ).start()

            @pl.when(jnp.logical_not(self_case))
            def _():
                pltpu.make_async_remote_copy(
                    src_ref=source.at[s],
                    dst_ref=place.at[y],
                    send_sem=send_sems.at[left_here],
                    recv_sem=recv_sems.at[arrived],
                    device_id=(x, yy, jnp.int32(cc), z),
                    device_id_type=MESH,
                ).start()

        def wait_recv():
            pltpu.make_async_copy(whole, whole, recv_sems.at[arrived]).wait()

        return wait_recv, wait_sent(y // 2 == c, bytes_of(source.at[0]), left_here)

    def half(ref, h):
        return ref.at[pl.ds(64 * h, 64)]

    class RowGather:
        def __init__(self, buf):
            self.left = buf.at[2 * plus(x, -1) + c]
            self.right = buf.at[2 * plus(x, 1) + c]
            self.far = buf.at[2 * plus(x, 2) + c]
            mine = buf.at[q]
            self.from_left = message(half(mine, 0), half(mine, 0), at_x(1))
            self.from_right = message(half(mine, 1), half(mine, 1), at_x(-1))
            self.rest = message(half(mine, 1), half(mine, 1), at_x(1))
            message(half(mine, 0), half(mine, 0), at_x(-1), self.rest)
            self.pair = message(mine, mine, partner)

        def pass_on(self):
            self.from_left.wait_recv()
            self.far_half = message(half(self.left, 0), half(self.left, 0), at_x(1))
            self.from_right.wait_recv()
            message(half(self.right, 1), half(self.right, 1), at_x(-1), self.far_half)

        def share(self):
            self.rest.wait_recv()
            message(self.left, self.left, partner, self.pair)
            message(self.right, self.right, partner, self.pair)

        def share_far(self):
            self.far_half.wait_recv()
            self.pair_far = message(self.far, self.far, partner)

    b_of = [plus(p_b, d) for d in order_a]
    halves = (pl.ds(0, 64), pl.ds(64, 64))

    a_far, a_next, a_prev, a_own = [plus(p_a, d) for d in order_a]
    relay_r, relay_l = [], []
    first_parts = [Arrivals() for _ in range(4)]
    for k in range(4):
        wait_part(k)
        add_part(a_far, b_of[k])
        relay_r.append(message(own.at[a_far, b_of[k], halves[0]], rec_a.at[0, k], at_a(1)))
        relay_l.append(message(own.at[a_far, b_of[k], halves[1]], rec_a.at[1, k], at_a(-1)))
    right_recv()
    gather_right = RowGather(right_full)
    wait_part(4)
    for k in range(4):
        add_part(a_next, b_of[k])
        message(own.at[a_next, b_of[k], halves[1]], rec_a.at[2, k], at_a(1), first_parts[k])
    wait_part(5)
    for k in range(4):
        add_part(a_prev, b_of[k])
        message(own.at[a_prev, b_of[k], halves[0]], rec_a.at[3, k], at_a(-1), first_parts[k])
    left_recv()
    mine = left_cols.at[q]
    tiles = Arrivals()
    for d in range(4):
        for e in range(2):
            xx, cc = plus(x, d), lax.rem(c + e, 2)
            columns = pl.ds(pl.multiple_of((2 * xx + cc) * 128, 128), 128)
            if d or e:
                message(left_rows.at[:, columns], mine, (xx, y, cc, z), tiles)
            else:
                own_tile = pltpu.make_async_copy(
                    left_rows.at[:, columns], mine, local_sems.at[10]
                )
                own_tile.start()

    wait_part(6)
    for k in range(4):
        add_part(a_own, b_of[k])

    for k in range(4):
        relay_r[k].wait_recv()
        own[a_next, b_of[k], 0:64, :] = own[a_next, b_of[k], 0:64, :] + rec_a[0, k]
        message(own.at[a_next, b_of[k], halves[0]], rec_a.at[4, k], at_a(1), first_parts[k])
        relay_l[k].wait_recv()
        own[a_prev, b_of[k], 64:128, :] = own[a_prev, b_of[k], 64:128, :] + rec_a[1, k]
        message(own.at[a_prev, b_of[k], halves[1]], rec_a.at[5, k], at_a(-1), first_parts[k])

    gather_right.pass_on()
    gather_right.share()

    for n, (ref, packed, m) in enumerate(
        ((first_in, moments_out, 0), (second_in, moments_out, 1), (master_in, master_out, None))
    ):
        pltpu.make_async_copy(ref, ref, local_sems.at[7 + n]).wait()

        @pl.loop(0, 4)
        def _(i):
            if m is None:
                packed[i] = ref[i].astype(BF16)
            else:
                packed[i, m] = ref[i].astype(BF16)

    moments_recv, moments_sent = to_block(
        lambda i: moments_out.at[i], moments_near.at[strip], moments_near
    )
    def sum_first(k):
        first_parts[k].wait_recv()
        own[a_own, b_of[k], 0:64, :] = (
            own[a_own, b_of[k], 0:64, :].astype(F32)
            + rec_a[3, k].astype(F32)
            + rec_a[4, k].astype(F32)
        ).astype(BF16)
        own[a_own, b_of[k], 64:128, :] = (
            own[a_own, b_of[k], 64:128, :].astype(F32)
            + rec_a[2, k].astype(F32)
            + rec_a[5, k].astype(F32)
        ).astype(BF16)

    sum_first(0)
    far = own.at[a_own, b_of[0]]
    second_relay_r = message(half(far, 0), rec_b.at[0], at_b(1))
    second_relay_l = message(half(far, 1), rec_b.at[1], at_b(-1))
    sum_first(1)
    second_parts = message(half(own.at[a_own, b_of[1]], 1), rec_b.at[2], at_b(1))
    sum_first(2)
    message(half(own.at[a_own, b_of[2]], 0), rec_b.at[3], at_b(-1), second_parts)
    second_relay_r.wait_recv()
    own[a_own, b_of[1], 0:64, :] = own[a_own, b_of[1], 0:64, :] + rec_b[0]
    message(half(own.at[a_own, b_of[1]], 0), rec_b.at[4], at_b(1), second_parts)
    second_relay_l.wait_recv()
    own[a_own, b_of[2], 64:128, :] = own[a_own, b_of[2], 64:128, :] + rec_b[1]
    message(half(own.at[a_own, b_of[2]], 1), rec_b.at[5], at_b(-1), second_parts)
    sum_first(3)
    gather_right.share_far()

    def sum_second(rows, one, two):
        total = jnp.zeros((8, 1024), F32)
        for r in range(0, 64, 16):
            at = pl.ds(rows + r, 16)
            part = pl.ds(r, 16)
            value = (
                own[a_own, p_b, at, :].astype(F32)
                + rec_b[one, part, :].astype(F32)
                + rec_b[two, part, :].astype(F32)
            )
            grad_low[at, :] = value.astype(BF16)
            total = total + (value * value).reshape(2, 8, 1024).sum(0)
        return total

    second_parts.wait_recv()
    total = sum_second(0, 3, 4) + sum_second(64, 2, 5)
    squares[0] = sum(total[:, 128 * k : 128 * (k + 1)] for k in range(8))
    over_row = message(squares.at[0], squares.at[1], partner)
    for d in (1, 2, 3):
        for n, cc in enumerate((c, 1 - c)):
            place = squares.at[2 * d + n]
            message(squares.at[0], place, (plus(x, d), y, cc, z), over_row)

    gather_right.pair.wait_recv()
    gather_right.pair_far.wait_recv()
    for n in range(4):
        columns = slice(256 * n, 256 * (n + 1))
        acc = jnp.zeros((128, 256), F32)
        for k in range(8):
            acc = acc + jnp.dot(
                grad_low[:, 128 * k : 128 * (k + 1)],
                right_full[k, :, columns],
                preferred_element_type=F32,
            )
        turned[q, :, columns] = acc.astype(BF16)
    gather_turned = RowGather(turned)
    over_row.wait_recv()
    squares[8] = sum(squares[n] for n in range(8))
    over_y, over_z = Arrivals(), Arrivals()
    for d in (1, 2, 3):
        message(squares.at[8], squares.at[8 + d], (x, plus(y, d), c, z), over_y)
    master_recv, master_sent = to_block(
        lambda i: master_out.at[i], master_near.at[strip], master_near
    )
    gather_turned.pass_on()
    over_y.wait_recv()
    squares[12] = sum(squares[n] for n in range(8, 12))
    for d in (1, 2, 3):
        message(squares.at[12], squares.at[12 + d], (x, y, c, plus(z, d)), over_z)
    gather_turned.share()
    own_tile.wait()
    tiles.wait_recv()
    gather_turned.pair.wait_recv()

    def rotated_from(chip, columns):
        pieces = pl.ds(2 * chip, 2)
        return lax.dot_general(
            left_cols[pieces].reshape(256, 128),
            turned[pieces, :, columns].reshape(256, 256),
            (((0,), (0,)), ((), ())),
            preferred_element_type=F32,
        )

    near = (x, plus(x, -1), plus(x, 1))
    for n in range(4):
        columns = slice(256 * n, 256 * (n + 1))
        sums[:, columns] = sum(rotated_from(chip, columns) for chip in near)
    gather_turned.share_far()
    over_z.wait_recv()
    total = sum(squares[n] for n in range(12, 16))
    squares_sum = jnp.sum(jnp.sum(total, axis=1, keepdims=True), axis=0, keepdims=True)
    clip_scale = jnp.minimum(1.0, 2.0 * D / jnp.sqrt(squares_sum + norm_epsilon))

    moments_recv()
    gather_turned.pair_far.wait_recv()
    bias_one = 1.0 - beta_one**STEP
    bias_two = 1.0 - beta_two**STEP

    def moments(clipped, m, v):
        return (
            beta_one * m + (1.0 - beta_one) * clipped,
            beta_two * v + (1.0 - beta_two) * clipped * clipped,
        )

    for n in range(4):
        columns = slice(256 * n, 256 * (n + 1))
        acc = sums[:, columns] + rotated_from(plus(x, 2), columns)
        for s in range(4):
            rows = acc[32 * s : 32 * (s + 1)]
            rotated_out[s, :, columns] = rows.astype(BF16)
            m, v = moments(
                clip_scale * rows,
                moments_near[s, 0, :, columns].astype(F32),
                moments_near[s, 1, :, columns].astype(F32),
            )
            direction[32 * s : 32 * (s + 1), columns] = (
                m / bias_one / (jnp.sqrt(v / bias_two) + epsilon)
            ).astype(BF16)

    for n in range(8):
        back[q, :, 128 * n : 128 * (n + 1)] = lax.dot_general(
            direction[...],
            right_full[n],
            (((1,), (1,)), ((), ())),
            preferred_element_type=F32,
        ).astype(BF16)
    gather_back = RowGather(back)
    rotated_recv, rotated_sent = to_owners(rotated_out, rotated_in, rotated_in)
    gather_back.pass_on()
    gather_back.share()

    rotated_recv()

    @pl.loop(0, 4)
    def _(i):
        m, v = moments(clip_scale * rotated_in[i].astype(F32), first_in[i], second_in[i])
        new_first[i] = m
        new_second[i] = v

    def update_from(chip, columns):
        pieces = pl.ds(2 * chip, 2)
        return jnp.dot(
            left_rows[:, pl.ds(pl.multiple_of(256 * chip, 256), 256)],
            back[pieces, :, columns].reshape(256, 256),
            preferred_element_type=F32,
        )

    master_recv()
    gather_back.pair.wait_recv()
    for n in range(4):
        columns = slice(256 * n, 256 * (n + 1))
        sums[:, columns] = sum(update_from(chip, columns) for chip in near)
    gather_back.share_far()
    gather_back.pair_far.wait_recv()

    def piece(a, b):
        return weights.at[jnp.where(is_x, b, a), 2 * jnp.where(is_x, a, b) + c]

    keep = 1.0 - learning_rate * decay_rate
    for n in range(4):
        columns = slice(256 * n, 256 * (n + 1))
        acc = sums[:, columns] + update_from(plus(x, 2), columns)
        for s in range(4):
            rows = acc[32 * s : 32 * (s + 1)]
            weights[y, q, 32 * s : 32 * (s + 1), columns] = (
                master_near[s, :, columns].astype(F32) * keep - learning_rate * rows
            ).astype(BF16)

    pair = Arrivals()

    def to_pair(ref):
        message(ref, ref, partner, pair)

    class Ring:
        def __init__(self, piece_at, at):
            self.prev, self.following, self.far = [piece_at(d) for d in (-1, 1, 2)]
            self.at = at
            piece = piece_at(0)
            self.up = message(half(piece, 0), half(piece, 0), at(1))
            self.down = message(half(piece, 1), half(piece, 1), at(-1))
            self.rest = message(half(piece, 1), half(piece, 1), at(1))
            message(half(piece, 0), half(piece, 0), at(-1), self.rest)

        def relay(self):
            self.up.wait_recv()
            piece = half(self.prev, 0)
            self.far_halves = message(piece, piece, self.at(1))
            self.down.wait_recv()
            piece = half(self.following, 1)
            message(piece, piece, self.at(-1), self.far_halves)

    def along_a(b):
        return Ring(lambda d: piece(plus(p_a, d), b), at_a)

    def share(ring):
        ring.rest.wait_recv()
        to_pair(ring.prev)
        to_pair(ring.following)

    def share_far(ring):
        ring.far_halves.wait_recv()
        to_pair(ring.far)

    ring_b = Ring(lambda d: piece(p_a, plus(p_b, d)), at_b)
    rings = [along_a(p_b)]
    to_pair(piece(p_a, p_b))
    ring_b.relay()
    rings[0].relay()
    share(ring_b)
    rings += [along_a(plus(p_b, -1)), along_a(plus(p_b, 1))]
    share_far(ring_b)
    rings.append(along_a(plus(p_b, 2)))
    share(rings[0])
    for n in (1, 2, 3):
        rings[n].relay()
        share_far(rings[n - 1])
        share(rings[n])
    share_far(rings[3])
    pair.wait_recv()

    @pl.loop(0, 4)
    def _(i):
        old = master_in[i]
        low = old.astype(BF16).astype(F32)
        new_master[i] = weights[i, 2 * x + h_own, place_rows, :].astype(F32) + keep * (old - low)

    for size, lots in send_lots.items():
        for index, copies in lots:
            wait_bytes(size * copies, send_sems.at[index])
    wait_bytes(4 * 256 * 1024, send_sems.at[swap_sent[0]])
    wait_bytes(3 * 1024 * 1024, send_sems.at[swap_sent[1]])
    right_sent()
    left_sent()
    moments_sent()
    master_sent()
    rotated_sent()
    assert used_send[0] <= N_SENDS and used_recv[0] <= N_ARRIVALS, (used_send, used_recv)


def write_kernel(a, b, c, d, a_out, b_out, c_out, d_out, sems):
    copies = [
        pltpu.make_async_copy(
            a.at[i, pl.ds(4 * j, 4)], a_out.at[i, pl.ds(4 * j, 4)], sems.at[2 * i + j]
        )
        for i in range(4)
        for j in range(2)
    ]
    for n, (source, place) in enumerate(((b, b_out), (c, c_out), (d, d_out))):
        copies.append(pltpu.make_async_copy(source, place, sems.at[8 + n]))
    for copy in copies:
        copy.start()
    for copy in copies:
        copy.wait()


def per_device(grad_parts, master, first_moment, second_moment, left_basis, right_basis):
    vmem = pl.BlockSpec(memory_space=pltpu.VMEM)
    hbm = pl.BlockSpec(memory_space=pltpu.HBM)
    state = pltpu.VMEM((4, 32, 1024), F32)
    outputs = pl.pallas_call(
        kernel,
        out_shape=(
            pltpu.VMEM((4, 8, 128, 1024), BF16),
            state,
            state,
            state,
        ),
        in_specs=[hbm] * 6,
        out_specs=(vmem, vmem, vmem, vmem),
        scratch_shapes=[
            pltpu.VMEM((4, 4, 128, 1024), BF16),
            pltpu.VMEM((4, 4, 128, 1024), BF16),
            pltpu.VMEM((6, 4, 64, 1024), BF16),
            pltpu.VMEM((6, 64, 1024), BF16),
            pltpu.VMEM((8, 128, 1024), BF16),
            pltpu.VMEM((128, 1024), BF16),
            pltpu.VMEM((8, 128, 128), BF16),
            pltpu.VMEM((8, 128, 1024), BF16),
            pltpu.VMEM((8, 128, 1024), BF16),
            pltpu.VMEM((4, 2, 32, 1024), BF16),
            pltpu.VMEM((4, 2, 32, 1024), BF16),
            pltpu.VMEM((4, 32, 1024), BF16),
            pltpu.VMEM((4, 32, 1024), BF16),
            pltpu.VMEM((4, 32, 1024), F32),
            pltpu.VMEM((4, 32, 1024), F32),
            pltpu.VMEM((4, 32, 1024), F32),
            pltpu.VMEM((128, 1024), BF16),
            pltpu.VMEM((128, 1024), BF16),
            pltpu.VMEM((4, 32, 1024), BF16),
            pltpu.VMEM((4, 32, 1024), BF16),
            pltpu.VMEM((128, 1024), F32),
            pltpu.VMEM((16, 8, 128), F32),
            pltpu.SemaphoreType.DMA((N_SENDS,)),
            pltpu.SemaphoreType.DMA((N_ARRIVALS,)),
            pltpu.SemaphoreType.DMA((11,)),
        ],
        compiler_params=pltpu.CompilerParams(
            collective_id=0, has_side_effects=True, vmem_limit_bytes=32 * 1024 * 1024
        ),
    )(
        *(
            pltpu.with_memory_space_constraint(array, pltpu.HBM)
            for array in (
                grad_parts.reshape(4, 4, 2, 128, 1024),
                master,
                first_moment,
                second_moment,
                left_basis,
                right_basis,
            )
        )
    )
    state = jax.ShapeDtypeStruct((4, 32, 1024), F32)
    weights, new_master, new_first, new_second = pl.pallas_call(
        write_kernel,
        out_shape=(jax.ShapeDtypeStruct((4, 8, 128, 1024), BF16), state, state, state),
        in_specs=[vmem] * 4,
        out_specs=(hbm, hbm, hbm, hbm),
        scratch_shapes=[pltpu.SemaphoreType.DMA((11,))],
        compiler_params=pltpu.CompilerParams(vmem_limit_bytes=4 * 1024 * 1024),
    )(*(pltpu.with_memory_space_constraint(array, pltpu.VMEM) for array in outputs))
    return (weights.reshape(4, 1024, 1024), new_master, new_first, new_second)


def solution(mesh):
    finer = Mesh(mesh.devices.reshape(4, 4, 2, mesh.shape["mp"]), ("dp_0", "dp_1", "dp_2", "mp"))
    placed = (
        P(DP, None, None, "mp"),
        P(None, DP, "mp"),
        P(None, DP, "mp"),
        P(None, DP, "mp"),
        P(None, DP, "mp"),
        P(None, DP, "mp"),
    )
    return jax.shard_map(
        per_device,
        mesh=finer,
        in_specs=placed,
        out_specs=(P(None, None, "mp"), P(None, DP, "mp"), P(None, DP, "mp"), P(None, DP, "mp")),
        check_vma=False,
    )
```

time: 110 us -> 105 us (0.955)
  Pallas kernels: 110 us -> 104 us
    pallas_call x1, Pallas kernels: 106 us -> 101 us  [per_device(): pl.pallas_call(kernel, out_shape=(pltpu.VMEM((4, 8, 128, 1024), BF16), st...]
where the time goes in v3:
time: 105 us
  Pallas kernels  104 us (99%)
    pallas_call x1, Pallas kernels, per_device(): pl.pallas_call(kernel, out_shape=(pltpu.VMEM((4, 8, 128, 1024), BF16), st...  101 us
    pallas_call x1, Pallas kernels, per_device(): pl.pallas_call(write_kernel, out_shape=(jax.ShapeDtypeStruct((4, 8, 128,...  3.85 us

profile of v3, /device:TPU:1, one launch (start us, length us, event | category | flops | bytes accessed | tf_op | source)
XLA Modules:
  0.0 105.1 jit_solution(2638917941403480590)
XLA Ops:
  0.6 100.6 %shard_map.93 = (bf16[4,8,128,1024]{3,2,1,0:T(8,128)(2,1)S(1)}, f32[4,32,1024]{2,1,0:T(8,128)S(1)}, f32[4,32,1024]{2,1,0:T(8,128)S(1)}, f32[4,32,1024]{2,1,0:T(8,128)S(1)}) custom-call(bf16[4,4,2,128,1024]{4,3,2,1,0:T(8,128)(2,1)} %bitcast.2, f32[4,32,1024]{2,1,0:T(8,128)} %master.1, f32[4,32,1024]{2,1,0:T(8,128)} %first.1, f32[4,32,1024]{2,1,0:T(8,128)} %second.1, ...), custom_call_target="tpu_custom_call" | custom-call | tf_op jit(solution)/shard_map/pallas_call | solution.py:642
  101.2 3.9 %shard_map.94 = (bf16[4,8,128,1024]{3,2,1,0:T(8,128)(2,1)}, f32[4,32,1024]{2,1,0:T(8,128)}, f32[4,32,1024]{2,1,0:T(8,128)}, f32[4,32,1024]{2,1,0:T(8,128)}) custom-call(bf16[4,8,128,1024]{3,2,1,0:T(8,128)(2,1)S(1)} %get-tuple-element.12.a, f32[4,32,1024]{2,1,0:T(8,128)S(1)} %get-tuple-element.13.b, f32[4,32,1024]{2,1,0:T(8,128)S(1)} %get-tuple-element.14.c, ...), custom_call_target="tpu_custom_call" | custom-call | tf_op jit(solution)/shard_map/pallas_call | solution.py:696
